TPU v7x, 32 devices: a whole 2x2x4 slice. The times are simulated.
32 devices in a mesh: row: 8 (over z, y), col: 4 (over x, core).
Axes of the slice: x: 2, y: 2, z: 4, core: 2. Of those that a mesh axis runs over, the one named last changes fastest.
Arguments:
- v_panels: float32 [4096, 4096], P('row', 'col')
- t_factors: float32 [128, 32, 32], P('col')
- z_vecs: float32 [4096, 4096], P(None, ('row', 'col'))
Outputs:
- output: float32 [4096, 4096], P(None, ('row', 'col'))
All inputs are finite; a program needn't handle non-finite values.
Results may differ from a plain program's by a relative error of at most 0.001.
Values sent between devices are 32-bit elements.
A program may use at most 1 GiB of HBM per device.

v0:
```python
import jax
import jax.numpy as jnp
from jax import lax
from jax.sharding import PartitionSpec as P, NamedSharding

FULL_PREC = lax.Precision.HIGHEST
CONTRACT_ROWS = (((0,), (0,)), ((), ()))


def solution(mesh):
    col_dev = mesh.shape["col"]

    def local_apply(v_loc, t_loc, z_loc):
        num_local = t_loc.shape[0]
        block_w = t_loc.shape[1]
        x_two = lax.all_to_all(z_loc, "row", 0, 1, tiled=True)

        def outer_step(step_idx, x_cur):
            local_idx = num_local - 1 - step_idx
            v_own = lax.dynamic_slice_in_dim(v_loc, local_idx * block_w, block_w, axis=1)
            t_own = lax.dynamic_index_in_dim(t_loc, local_idx, axis=0, keepdims=False)
            v_all = lax.all_gather(v_own, "col")
            t_all = lax.all_gather(t_own, "col")

            def inner_step(sub_idx, x_in):
                owner_col = col_dev - 1 - sub_idx
                v_blk = v_all[owner_col]
                t_blk = t_all[owner_col]
                w_part = lax.dot_general(v_blk, x_in, CONTRACT_ROWS, precision=FULL_PREC, preferred_element_type=jnp.float32)
                w_sum = lax.psum(w_part, "row")
                y_blk = jnp.dot(t_blk, w_sum, precision=FULL_PREC, preferred_element_type=jnp.float32)
                return x_in - jnp.dot(v_blk, y_blk, precision=FULL_PREC, preferred_element_type=jnp.float32)

            return lax.fori_loop(0, col_dev, inner_step, x_cur)

        x_two = lax.fori_loop(0, num_local, outer_step, x_two)
        return lax.all_to_all(x_two, "row", 1, 0, tiled=True)

    return jax.shard_map(
        local_apply,
        mesh=mesh,
        in_specs=(P("row", "col"), P("col", None, None), P(None, ("row", "col"))),
        out_specs=P(None, ("row", "col")),
        check_vma=False,
    )
```

profile of v0, /device:TPU:17, one launch (start us, length us, event | category | flops | bytes accessed | tf_op | source)
XLA Modules:
  0.0 10494.1 jit_solution(16771853011163242450)
XLA Ops:
  59.7 10374.2 %while.44 = (s32[]{:T(128)}, f32[512,1024]{1,0:T(8,128)S(1)}, f32[512,1024]{1,0:T(8,128)}, f32[32,32,32]{2,1,0:T(8,128)}, s32[]{:T(128)}, /*index=5*/s32[]{:T(12...) while((s32[]{:T(128)}, f32[512,1024]{1,0:T(8,128)S(1)}, ...), condition=%wide.region_4.5_spmd, body=%wide.region_0.4_spmd.sunk | while | flops 415793152 | bytes 8630768 | solution.py:36
  79.1 306.9 %while.45 = (s32[]{:T(128)}, f32[512,1024]{1,0:T(8,128)S(1)}, f32[4,512,32]{2,1,0:T(8,128)S(1)}, f32[4,32,32]{2,1,0:T(8,128)S(1)}, s32[]{:T(128)}, /*index=5*/s32[]{:T(128)}, s32[]{:T(128)}, s32[]{:T(128)}) while((s32[]{:T(128)}, f32[512,1024]{1,0:T(8,128)S(1)}, f32[4,512,32]{2,1,0:T(8,128)S(1)}, f32[4,32,32]{2,1,0:T(8,128)S(1)}, s32[]{:T(128)}, ...), condition=%wide.region_3.3_spmd, body=%wide.region_1.2_spmd.sunk | while | flops 415793152 | bytes 8143031 | solution.py:34
  157.7 71.5 all-reduce.2.cloned.1.call-done
  405.6 304.6 %while.45 = (s32[]{:T(128)}, f32[512,1024]{1,0:T(8,128)S(1)}, f32[4,512,32]{2,1,0:T(8,128)S(1)}, f32[4,32,32]{2,1,0:T(8,128)S(1)}, s32[]{:T(128)}, /*index=5*/s32[]{:T(128)}, s32[]{:T(128)}, s32[]{:T(128)}) while((s32[]{:T(128)}, f32[512,1024]{1,0:T(8,128)S(1)}, f32[4,512,32]{2,1,0:T(8,128)S(1)}, f32[4,32,32]{2,1,0:T(8,128)S(1)}, s32[]{:T(128)}, ...), condition=%wide.region_3.3_spmd, body=%wide.region_1.2_spmd.sunk | while | flops 415793152 | bytes 8143031 | solution.py:34
  558.4 71.5 all-reduce.2.cloned.1.call-done
  635.3 71.5 all-reduce.2.cloned.1.call-done
  729.7 304.6 %while.45 = (s32[]{:T(128)}, f32[512,1024]{1,0:T(8,128)S(1)}, f32[4,512,32]{2,1,0:T(8,128)S(1)}, f32[4,32,32]{2,1,0:T(8,128)S(1)}, s32[]{:T(128)}, /*index=5*/s32[]{:T(128)}, s32[]{:T(128)}, s32[]{:T(128)}) while((s32[]{:T(128)}, f32[512,1024]{1,0:T(8,128)S(1)}, f32[4,512,32]{2,1,0:T(8,128)S(1)}, f32[4,32,32]{2,1,0:T(8,128)S(1)}, s32[]{:T(128)}, ...), condition=%wide.region_3.3_spmd, body=%wide.region_1.2_spmd.sunk | while | flops 415793152 | bytes 8143031 | solution.py:34
  882.9 71.5 all-reduce.2.cloned.1.call-done
  1053.8 304.3 %while.45 = (s32[]{:T(128)}, f32[512,1024]{1,0:T(8,128)S(1)}, f32[4,512,32]{2,1,0:T(8,128)S(1)}, f32[4,32,32]{2,1,0:T(8,128)S(1)}, s32[]{:T(128)}, /*index=5*/s32[]{:T(128)}, s32[]{:T(128)}, s32[]{:T(128)}) while((s32[]{:T(128)}, f32[512,1024]{1,0:T(8,128)S(1)}, f32[4,512,32]{2,1,0:T(8,128)S(1)}, f32[4,32,32]{2,1,0:T(8,128)S(1)}, s32[]{:T(128)}, ...), condition=%wide.region_3.3_spmd, body=%wide.region_1.2_spmd.sunk | while | flops 415793152 | bytes 8143031 | solution.py:34
  1377.7 304.2 %while.45 = (s32[]{:T(128)}, f32[512,1024]{1,0:T(8,128)S(1)}, f32[4,512,32]{2,1,0:T(8,128)S(1)}, f32[4,32,32]{2,1,0:T(8,128)S(1)}, s32[]{:T(128)}, /*index=5*/s32[]{:T(128)}, s32[]{:T(128)}, s32[]{:T(128)}) while((s32[]{:T(128)}, f32[512,1024]{1,0:T(8,128)S(1)}, f32[4,512,32]{2,1,0:T(8,128)S(1)}, f32[4,32,32]{2,1,0:T(8,128)S(1)}, s32[]{:T(128)}, ...), condition=%wide.region_3.3_spmd, body=%wide.region_1.2_spmd.sunk | while | flops 415793152 | bytes 8143031 | solution.py:34
  1701.5 304.9 %while.45 = (s32[]{:T(128)}, f32[512,1024]{1,0:T(8,128)S(1)}, f32[4,512,32]{2,1,0:T(8,128)S(1)}, f32[4,32,32]{2,1,0:T(8,128)S(1)}, s32[]{:T(128)}, /*index=5*/s32[]{:T(128)}, s32[]{:T(128)}, s32[]{:T(128)}) while((s32[]{:T(128)}, f32[512,1024]{1,0:T(8,128)S(1)}, f32[4,512,32]{2,1,0:T(8,128)S(1)}, f32[4,32,32]{2,1,0:T(8,128)S(1)}, s32[]{:T(128)}, ...), condition=%wide.region_3.3_spmd, body=%wide.region_1.2_spmd.sunk | while | flops 415793152 | bytes 8143031 | solution.py:34
  1778.0 71.5 all-reduce.2.cloned.1.call-done
  1854.9 71.5 all-reduce.2.cloned.1.call-done
  2025.9 304.5 %while.45 = (s32[]{:T(128)}, f32[512,1024]{1,0:T(8,128)S(1)}, f32[4,512,32]{2,1,0:T(8,128)S(1)}, f32[4,32,32]{2,1,0:T(8,128)S(1)}, s32[]{:T(128)}, /*index=5*/s32[]{:T(128)}, s32[]{:T(128)}, s32[]{:T(128)}) while((s32[]{:T(128)}, f32[512,1024]{1,0:T(8,128)S(1)}, f32[4,512,32]{2,1,0:T(8,128)S(1)}, f32[4,32,32]{2,1,0:T(8,128)S(1)}, s32[]{:T(128)}, ...), condition=%wide.region_3.3_spmd, body=%wide.region_1.2_spmd.sunk | while | flops 415793152 | bytes 8143031 | solution.py:34
  2255.6 71.5 all-reduce.2.cloned.1.call-done
  2350.0 304.8 %while.45 = (s32[]{:T(128)}, f32[512,1024]{1,0:T(8,128)S(1)}, f32[4,512,32]{2,1,0:T(8,128)S(1)}, f32[4,32,32]{2,1,0:T(8,128)S(1)}, s32[]{:T(128)}, /*index=5*/s32[]{:T(128)}, s32[]{:T(128)}, s32[]{:T(128)}) while((s32[]{:T(128)}, f32[512,1024]{1,0:T(8,128)S(1)}, f32[4,512,32]{2,1,0:T(8,128)S(1)}, f32[4,32,32]{2,1,0:T(8,128)S(1)}, s32[]{:T(128)}, ...), condition=%wide.region_3.3_spmd, body=%wide.region_1.2_spmd.sunk | while | flops 415793152 | bytes 8143031 | solution.py:34
  2674.4 304.5 %while.45 = (s32[]{:T(128)}, f32[512,1024]{1,0:T(8,128)S(1)}, f32[4,512,32]{2,1,0:T(8,128)S(1)}, f32[4,32,32]{2,1,0:T(8,128)S(1)}, s32[]{:T(128)}, /*index=5*/s32[]{:T(128)}, s32[]{:T(128)}, s32[]{:T(128)}) while((s32[]{:T(128)}, f32[512,1024]{1,0:T(8,128)S(1)}, f32[4,512,32]{2,1,0:T(8,128)S(1)}, f32[4,32,32]{2,1,0:T(8,128)S(1)}, s32[]{:T(128)}, ...), condition=%wide.region_3.3_spmd, body=%wide.region_1.2_spmd.sunk | while | flops 415793152 | bytes 8143031 | solution.py:34
  2750.6 71.5 all-reduce.2.cloned.1.call-done
  2998.4 304.6 %while.45 = (s32[]{:T(128)}, f32[512,1024]{1,0:T(8,128)S(1)}, f32[4,512,32]{2,1,0:T(8,128)S(1)}, f32[4,32,32]{2,1,0:T(8,128)S(1)}, s32[]{:T(128)}, /*index=5*/s32[]{:T(128)}, s32[]{:T(128)}, s32[]{:T(128)}) while((s32[]{:T(128)}, f32[512,1024]{1,0:T(8,128)S(1)}, f32[4,512,32]{2,1,0:T(8,128)S(1)}, f32[4,32,32]{2,1,0:T(8,128)S(1)}, s32[]{:T(128)}, ...), condition=%wide.region_3.3_spmd, body=%wide.region_1.2_spmd.sunk | while | flops 415793152 | bytes 8143031 | solution.py:34
  3074.7 71.5 all-reduce.2.cloned.1.call-done
  3322.6 304.9 %while.45 = (s32[]{:T(128)}, f32[512,1024]{1,0:T(8,128)S(1)}, f32[4,512,32]{2,1,0:T(8,128)S(1)}, f32[4,32,32]{2,1,0:T(8,128)S(1)}, s32[]{:T(128)}, /*index=5*/s32[]{:T(128)}, s32[]{:T(128)}, s32[]{:T(128)}) while((s32[]{:T(128)}, f32[512,1024]{1,0:T(8,128)S(1)}, f32[4,512,32]{2,1,0:T(8,128)S(1)}, f32[4,32,32]{2,1,0:T(8,128)S(1)}, s32[]{:T(128)}, ...), condition=%wide.region_3.3_spmd, body=%wide.region_1.2_spmd.sunk | while | flops 415793152 | bytes 8143031 | solution.py:34
  3399.2 71.5 all-reduce.2.cloned.1.call-done
  3552.6 71.5 all-reduce.2.cloned.1.call-done
  3647.0 303.9 %while.45 = (s32[]{:T(128)}, f32[512,1024]{1,0:T(8,128)S(1)}, f32[4,512,32]{2,1,0:T(8,128)S(1)}, f32[4,32,32]{2,1,0:T(8,128)S(1)}, s32[]{:T(128)}, /*index=5*/s32[]{:T(128)}, s32[]{:T(128)}, s32[]{:T(128)}) while((s32[]{:T(128)}, f32[512,1024]{1,0:T(8,128)S(1)}, f32[4,512,32]{2,1,0:T(8,128)S(1)}, f32[4,32,32]{2,1,0:T(8,128)S(1)}, s32[]{:T(128)}, ...), condition=%wide.region_3.3_spmd, body=%wide.region_1.2_spmd.sunk | while | flops 415793152 | bytes 8143031 | solution.py:34
  3970.5 304.6 %while.45 = (s32[]{:T(128)}, f32[512,1024]{1,0:T(8,128)S(1)}, f32[4,512,32]{2,1,0:T(8,128)S(1)}, f32[4,32,32]{2,1,0:T(8,128)S(1)}, s32[]{:T(128)}, /*index=5*/s32[]{:T(128)}, s32[]{:T(128)}, s32[]{:T(128)}) while((s32[]{:T(128)}, f32[512,1024]{1,0:T(8,128)S(1)}, f32[4,512,32]{2,1,0:T(8,128)S(1)}, f32[4,32,32]{2,1,0:T(8,128)S(1)}, s32[]{:T(128)}, ...), condition=%wide.region_3.3_spmd, body=%wide.region_1.2_spmd.sunk | while | flops 415793152 | bytes 8143031 | solution.py:34
  4046.8 71.5 all-reduce.2.cloned.1.call-done
  4200.3 71.5 all-reduce.2.cloned.1.call-done
  4294.7 304.8 %while.45 = (s32[]{:T(128)}, f32[512,1024]{1,0:T(8,128)S(1)}, f32[4,512,32]{2,1,0:T(8,128)S(1)}, f32[4,32,32]{2,1,0:T(8,128)S(1)}, s32[]{:T(128)}, /*index=5*/s32[]{:T(128)}, s32[]{:T(128)}, s32[]{:T(128)}) while((s32[]{:T(128)}, f32[512,1024]{1,0:T(8,128)S(1)}, f32[4,512,32]{2,1,0:T(8,128)S(1)}, f32[4,32,32]{2,1,0:T(8,128)S(1)}, s32[]{:T(128)}, ...), condition=%wide.region_3.3_spmd, body=%wide.region_1.2_spmd.sunk | while | flops 415793152 | bytes 8143031 | solution.py:34
  4370.9 71.5 all-reduce.2.cloned.1.call-done
  4619.1 304.5 %while.45 = (s32[]{:T(128)}, f32[512,1024]{1,0:T(8,128)S(1)}, f32[4,512,32]{2,1,0:T(8,128)S(1)}, f32[4,32,32]{2,1,0:T(8,128)S(1)}, s32[]{:T(128)}, /*index=5*/s32[]{:T(128)}, s32[]{:T(128)}, s32[]{:T(128)}) while((s32[]{:T(128)}, f32[512,1024]{1,0:T(8,128)S(1)}, f32[4,512,32]{2,1,0:T(8,128)S(1)}, f32[4,32,32]{2,1,0:T(8,128)S(1)}, s32[]{:T(128)}, ...), condition=%wide.region_3.3_spmd, body=%wide.region_1.2_spmd.sunk | while | flops 415793152 | bytes 8143031 | solution.py:34
  4943.1 304.6 %while.45 = (s32[]{:T(128)}, f32[512,1024]{1,0:T(8,128)S(1)}, f32[4,512,32]{2,1,0:T(8,128)S(1)}, f32[4,32,32]{2,1,0:T(8,128)S(1)}, s32[]{:T(128)}, /*index=5*/s32[]{:T(128)}, s32[]{:T(128)}, s32[]{:T(128)}) while((s32[]{:T(128)}, f32[512,1024]{1,0:T(8,128)S(1)}, f32[4,512,32]{2,1,0:T(8,128)S(1)}, f32[4,32,32]{2,1,0:T(8,128)S(1)}, s32[]{:T(128)}, ...), condition=%wide.region_3.3_spmd, body=%wide.region_1.2_spmd.sunk | while | flops 415793152 | bytes 8143031 | solution.py:34
  5019.7 71.5 all-reduce.2.cloned.1.call-done
  5267.3 304.6 %while.45 = (s32[]{:T(128)}, f32[512,1024]{1,0:T(8,128)S(1)}, f32[4,512,32]{2,1,0:T(8,128)S(1)}, f32[4,32,32]{2,1,0:T(8,128)S(1)}, s32[]{:T(128)}, /*index=5*/s32[]{:T(128)}, s32[]{:T(128)}, s32[]{:T(128)}) while((s32[]{:T(128)}, f32[512,1024]{1,0:T(8,128)S(1)}, f32[4,512,32]{2,1,0:T(8,128)S(1)}, f32[4,32,32]{2,1,0:T(8,128)S(1)}, s32[]{:T(128)}, ...), condition=%wide.region_3.3_spmd, body=%wide.region_1.2_spmd.sunk | while | flops 415793152 | bytes 8143031 | solution.py:34
  5591.4 304.6 %while.45 = (s32[]{:T(128)}, f32[512,1024]{1,0:T(8,128)S(1)}, f32[4,512,32]{2,1,0:T(8,128)S(1)}, f32[4,32,32]{2,1,0:T(8,128)S(1)}, s32[]{:T(128)}, /*index=5*/s32[]{:T(128)}, s32[]{:T(128)}, s32[]{:T(128)}) while((s32[]{:T(128)}, f32[512,1024]{1,0:T(8,128)S(1)}, f32[4,512,32]{2,1,0:T(8,128)S(1)}, f32[4,32,32]{2,1,0:T(8,128)S(1)}, s32[]{:T(128)}, ...), condition=%wide.region_3.3_spmd, body=%wide.region_1.2_spmd.sunk | while | flops 415793152 | bytes 8143031 | solution.py:34
  5915.5 304.2 %while.45 = (s32[]{:T(128)}, f32[512,1024]{1,0:T(8,128)S(1)}, f32[4,512,32]{2,1,0:T(8,128)S(1)}, f32[4,32,32]{2,1,0:T(8,128)S(1)}, s32[]{:T(128)}, /*index=5*/s32[]{:T(128)}, s32[]{:T(128)}, s32[]{:T(128)}) while((s32[]{:T(128)}, f32[512,1024]{1,0:T(8,128)S(1)}, f32[4,512,32]{2,1,0:T(8,128)S(1)}, f32[4,32,32]{2,1,0:T(8,128)S(1)}, s32[]{:T(128)}, ...), condition=%wide.region_3.3_spmd, body=%wide.region_1.2_spmd.sunk | while | flops 415793152 | bytes 8143031 | solution.py:34
  6239.3 305.2 %while.45 = (s32[]{:T(128)}, f32[512,1024]{1,0:T(8,128)S(1)}, f32[4,512,32]{2,1,0:T(8,128)S(1)}, f32[4,32,32]{2,1,0:T(8,128)S(1)}, s32[]{:T(128)}, /*index=5*/s32[]{:T(128)}, s32[]{:T(128)}, s32[]{:T(128)}) while((s32[]{:T(128)}, f32[512,1024]{1,0:T(8,128)S(1)}, f32[4,512,32]{2,1,0:T(8,128)S(1)}, f32[4,32,32]{2,1,0:T(8,128)S(1)}, s32[]{:T(128)}, ...), condition=%wide.region_3.3_spmd, body=%wide.region_1.2_spmd.sunk | while | flops 415793152 | bytes 8143031 | solution.py:34
  6469.6 71.5 all-reduce.2.cloned.1.call-done
  6564.0 304.6 %while.45 = (s32[]{:T(128)}, f32[512,1024]{1,0:T(8,128)S(1)}, f32[4,512,32]{2,1,0:T(8,128)S(1)}, f32[4,32,32]{2,1,0:T(8,128)S(1)}, s32[]{:T(128)}, /*index=5*/s32[]{:T(128)}, s32[]{:T(128)}, s32[]{:T(128)}) while((s32[]{:T(128)}, f32[512,1024]{1,0:T(8,128)S(1)}, f32[4,512,32]{2,1,0:T(8,128)S(1)}, f32[4,32,32]{2,1,0:T(8,128)S(1)}, s32[]{:T(128)}, ...), condition=%wide.region_3.3_spmd, body=%wide.region_1.2_spmd.sunk | while | flops 415793152 | bytes 8143031 | solution.py:34
  6717.2 71.5 all-reduce.2.cloned.1.call-done
  6888.1 304.3 %while.45 = (s32[]{:T(128)}, f32[512,1024]{1,0:T(8,128)S(1)}, f32[4,512,32]{2,1,0:T(8,128)S(1)}, f32[4,32,32]{2,1,0:T(8,128)S(1)}, s32[]{:T(128)}, /*index=5*/s32[]{:T(128)}, s32[]{:T(128)}, s32[]{:T(128)}) while((s32[]{:T(128)}, f32[512,1024]{1,0:T(8,128)S(1)}, f32[4,512,32]{2,1,0:T(8,128)S(1)}, f32[4,32,32]{2,1,0:T(8,128)S(1)}, s32[]{:T(128)}, ...), condition=%wide.region_3.3_spmd, body=%wide.region_1.2_spmd.sunk | while | flops 415793152 | bytes 8143031 | solution.py:34
  7212.0 304.9 %while.45 = (s32[]{:T(128)}, f32[512,1024]{1,0:T(8,128)S(1)}, f32[4,512,32]{2,1,0:T(8,128)S(1)}, f32[4,32,32]{2,1,0:T(8,128)S(1)}, s32[]{:T(128)}, /*index=5*/s32[]{:T(128)}, s32[]{:T(128)}, s32[]{:T(128)}) while((s32[]{:T(128)}, f32[512,1024]{1,0:T(8,128)S(1)}, f32[4,512,32]{2,1,0:T(8,128)S(1)}, f32[4,32,32]{2,1,0:T(8,128)S(1)}, s32[]{:T(128)}, ...), condition=%wide.region_3.3_spmd, body=%wide.region_1.2_spmd.sunk | while | flops 415793152 | bytes 8143031 | solution.py:34
  7288.5 71.5 all-reduce.2.cloned.1.call-done
  7536.4 304.9 %while.45 = (s32[]{:T(128)}, f32[512,1024]{1,0:T(8,128)S(1)}, f32[4,512,32]{2,1,0:T(8,128)S(1)}, f32[4,32,32]{2,1,0:T(8,128)S(1)}, s32[]{:T(128)}, /*index=5*/s32[]{:T(128)}, s32[]{:T(128)}, s32[]{:T(128)}) while((s32[]{:T(128)}, f32[512,1024]{1,0:T(8,128)S(1)}, f32[4,512,32]{2,1,0:T(8,128)S(1)}, f32[4,32,32]{2,1,0:T(8,128)S(1)}, s32[]{:T(128)}, ...), condition=%wide.region_3.3_spmd, body=%wide.region_1.2_spmd.sunk | while | flops 415793152 | bytes 8143031 | solution.py:34
  7612.7 71.5 all-reduce.2.cloned.1.call-done
  7689.6 71.5 all-reduce.2.cloned.1.call-done
  7766.5 71.5 all-reduce.2.cloned.1.call-done
  7860.8 303.9 %while.45 = (s32[]{:T(128)}, f32[512,1024]{1,0:T(8,128)S(1)}, f32[4,512,32]{2,1,0:T(8,128)S(1)}, f32[4,32,32]{2,1,0:T(8,128)S(1)}, s32[]{:T(128)}, /*index=5*/s32[]{:T(128)}, s32[]{:T(128)}, s32[]{:T(128)}) while((s32[]{:T(128)}, f32[512,1024]{1,0:T(8,128)S(1)}, f32[4,512,32]{2,1,0:T(8,128)S(1)}, f32[4,32,32]{2,1,0:T(8,128)S(1)}, s32[]{:T(128)}, ...), condition=%wide.region_3.3_spmd, body=%wide.region_1.2_spmd.sunk | while | flops 415793152 | bytes 8143031 | solution.py:34
  8184.3 304.6 %while.45 = (s32[]{:T(128)}, f32[512,1024]{1,0:T(8,128)S(1)}, f32[4,512,32]{2,1,0:T(8,128)S(1)}, f32[4,32,32]{2,1,0:T(8,128)S(1)}, s32[]{:T(128)}, /*index=5*/s32[]{:T(128)}, s32[]{:T(128)}, s32[]{:T(128)}) while((s32[]{:T(128)}, f32[512,1024]{1,0:T(8,128)S(1)}, f32[4,512,32]{2,1,0:T(8,128)S(1)}, f32[4,32,32]{2,1,0:T(8,128)S(1)}, s32[]{:T(128)}, ...), condition=%wide.region_3.3_spmd, body=%wide.region_1.2_spmd.sunk | while | flops 415793152 | bytes 8143031 | solution.py:34
  8260.9 71.5 all-reduce.2.cloned.1.call-done
  8508.5 304.6 %while.45 = (s32[]{:T(128)}, f32[512,1024]{1,0:T(8,128)S(1)}, f32[4,512,32]{2,1,0:T(8,128)S(1)}, f32[4,32,32]{2,1,0:T(8,128)S(1)}, s32[]{:T(128)}, /*index=5*/s32[]{:T(128)}, s32[]{:T(128)}, s32[]{:T(128)}) while((s32[]{:T(128)}, f32[512,1024]{1,0:T(8,128)S(1)}, f32[4,512,32]{2,1,0:T(8,128)S(1)}, f32[4,32,32]{2,1,0:T(8,128)S(1)}, s32[]{:T(128)}, ...), condition=%wide.region_3.3_spmd, body=%wide.region_1.2_spmd.sunk | while | flops 415793152 | bytes 8143031 | solution.py:34
  8584.7 71.5 all-reduce.2.cloned.1.call-done
  8738.2 71.5 all-reduce.2.cloned.1.call-done
  8832.6 304.8 %while.45 = (s32[]{:T(128)}, f32[512,1024]{1,0:T(8,128)S(1)}, f32[4,512,32]{2,1,0:T(8,128)S(1)}, f32[4,32,32]{2,1,0:T(8,128)S(1)}, s32[]{:T(128)}, /*index=5*/s32[]{:T(128)}, s32[]{:T(128)}, s32[]{:T(128)}) while((s32[]{:T(128)}, f32[512,1024]{1,0:T(8,128)S(1)}, f32[4,512,32]{2,1,0:T(8,128)S(1)}, f32[4,32,32]{2,1,0:T(8,128)S(1)}, s32[]{:T(128)}, ...), condition=%wide.region_3.3_spmd, body=%wide.region_1.2_spmd.sunk | while | flops 415793152 | bytes 8143031 | solution.py:34
  8908.9 71.5 all-reduce.2.cloned.1.call-done
  9157.0 304.9 %while.45 = (s32[]{:T(128)}, f32[512,1024]{1,0:T(8,128)S(1)}, f32[4,512,32]{2,1,0:T(8,128)S(1)}, f32[4,32,32]{2,1,0:T(8,128)S(1)}, s32[]{:T(128)}, /*index=5*/s32[]{:T(128)}, s32[]{:T(128)}, s32[]{:T(128)}) while((s32[]{:T(128)}, f32[512,1024]{1,0:T(8,128)S(1)}, f32[4,512,32]{2,1,0:T(8,128)S(1)}, f32[4,32,32]{2,1,0:T(8,128)S(1)}, s32[]{:T(128)}, ...), condition=%wide.region_3.3_spmd, body=%wide.region_1.2_spmd.sunk | while | flops 415793152 | bytes 8143031 | solution.py:34
  9233.6 71.5 all-reduce.2.cloned.1.call-done
  9387.0 71.5 all-reduce.2.cloned.1.call-done
  9481.4 304.2 %while.45 = (s32[]{:T(128)}, f32[512,1024]{1,0:T(8,128)S(1)}, f32[4,512,32]{2,1,0:T(8,128)S(1)}, f32[4,32,32]{2,1,0:T(8,128)S(1)}, s32[]{:T(128)}, /*index=5*/s32[]{:T(128)}, s32[]{:T(128)}, s32[]{:T(128)}) while((s32[]{:T(128)}, f32[512,1024]{1,0:T(8,128)S(1)}, f32[4,512,32]{2,1,0:T(8,128)S(1)}, f32[4,32,32]{2,1,0:T(8,128)S(1)}, s32[]{:T(128)}, ...), condition=%wide.region_3.3_spmd, body=%wide.region_1.2_spmd.sunk | while | flops 415793152 | bytes 8143031 | solution.py:34
  9710.8 71.5 all-reduce.2.cloned.1.call-done
  9805.2 304.6 %while.45 = (s32[]{:T(128)}, f32[512,1024]{1,0:T(8,128)S(1)}, f32[4,512,32]{2,1,0:T(8,128)S(1)}, f32[4,32,32]{2,1,0:T(8,128)S(1)}, s32[]{:T(128)}, /*index=5*/s32[]{:T(128)}, s32[]{:T(128)}, s32[]{:T(128)}) while((s32[]{:T(128)}, f32[512,1024]{1,0:T(8,128)S(1)}, f32[4,512,32]{2,1,0:T(8,128)S(1)}, f32[4,32,32]{2,1,0:T(8,128)S(1)}, s32[]{:T(128)}, ...), condition=%wide.region_3.3_spmd, body=%wide.region_1.2_spmd.sunk | while | flops 415793152 | bytes 8143031 | solution.py:34
  9881.5 71.5 all-reduce.2.cloned.1.call-done
  9958.4 71.5 all-reduce.2.cloned.1.call-done
  10129.3 304.6 %while.45 = (s32[]{:T(128)}, f32[512,1024]{1,0:T(8,128)S(1)}, f32[4,512,32]{2,1,0:T(8,128)S(1)}, f32[4,32,32]{2,1,0:T(8,128)S(1)}, s32[]{:T(128)}, /*index=5*/s32[]{:T(128)}, s32[]{:T(128)}, s32[]{:T(128)}) while((s32[]{:T(128)}, f32[512,1024]{1,0:T(8,128)S(1)}, f32[4,512,32]{2,1,0:T(8,128)S(1)}, f32[4,32,32]{2,1,0:T(8,128)S(1)}, s32[]{:T(128)}, ...), condition=%wide.region_3.3_spmd, body=%wide.region_1.2_spmd.sunk | while | flops 415793152 | bytes 8143031 | solution.py:34
  10205.6 71.5 all-reduce.2.cloned.1.call-done
  (872 shorter events, 8256.3 us)
Async XLA Ops:
  155.6 73.6 all-reduce.2.cloned.1.call-start
  232.6 73.6 all-reduce.2.cloned.1.call-start
  556.4 73.6 all-reduce.2.cloned.1.call-start
  633.3 73.6 all-reduce.2.cloned.1.call-start
  804.2 73.3 all-reduce.2.cloned.1.call-start
  880.8 73.6 all-reduce.2.cloned.1.call-start
  1204.9 73.3 all-reduce.2.cloned.1.call-start
  1451.9 73.3 all-reduce.2.cloned.1.call-start
  1528.5 73.6 all-reduce.2.cloned.1.call-start
  1776.0 73.6 all-reduce.2.cloned.1.call-start
  1852.9 73.6 all-reduce.2.cloned.1.call-start
  2253.5 73.6 all-reduce.2.cloned.1.call-start
  2424.5 73.3 all-reduce.2.cloned.1.call-start
  2501.1 73.6 all-reduce.2.cloned.1.call-start
  2577.9 73.5 all-reduce.2.cloned.1.call-start
  2748.6 73.6 all-reduce.2.cloned.1.call-start
  2825.4 73.6 all-reduce.2.cloned.1.call-start
  3072.6 73.6 all-reduce.2.cloned.1.call-start
  3149.5 73.3 all-reduce.2.cloned.1.call-start
  3226.2 73.5 all-reduce.2.cloned.1.call-start
  3397.1 73.6 all-reduce.2.cloned.1.call-start
  3550.6 73.6 all-reduce.2.cloned.1.call-start
  3874.4 73.3 all-reduce.2.cloned.1.call-start
  4044.7 73.6 all-reduce.2.cloned.1.call-start
  4198.2 73.6 all-reduce.2.cloned.1.call-start
  4368.8 73.6 all-reduce.2.cloned.1.call-start
  4445.7 73.6 all-reduce.2.cloned.1.call-start
  4522.6 73.6 all-reduce.2.cloned.1.call-start
  4693.5 73.3 all-reduce.2.cloned.1.call-start
  4846.7 73.5 all-reduce.2.cloned.1.call-start
  5017.6 73.6 all-reduce.2.cloned.1.call-start
  5094.5 73.3 all-reduce.2.cloned.1.call-start
  5341.8 73.3 all-reduce.2.cloned.1.call-start
  5495.0 73.6 all-reduce.2.cloned.1.call-start
  5742.5 73.5 all-reduce.2.cloned.1.call-start
  6066.2 73.6 all-reduce.2.cloned.1.call-start
  6313.8 73.6 all-reduce.2.cloned.1.call-start
  6390.7 73.5 all-reduce.2.cloned.1.call-start
  6467.5 73.6 all-reduce.2.cloned.1.call-start
  6638.5 73.3 all-reduce.2.cloned.1.call-start
  6715.1 73.6 all-reduce.2.cloned.1.call-start
  7039.2 73.3 all-reduce.2.cloned.1.call-start
  7115.8 73.3 all-reduce.2.cloned.1.call-start
  7286.5 73.6 all-reduce.2.cloned.1.call-start
  7363.4 73.6 all-reduce.2.cloned.1.call-start
  7610.6 73.6 all-reduce.2.cloned.1.call-start
  7687.5 73.6 all-reduce.2.cloned.1.call-start
  7764.4 73.6 all-reduce.2.cloned.1.call-start
  8011.6 73.3 all-reduce.2.cloned.1.call-start
  8258.8 73.6 all-reduce.2.cloned.1.call-start
  8412.3 73.3 all-reduce.2.cloned.1.call-start
  8582.7 73.6 all-reduce.2.cloned.1.call-start
  8736.2 73.6 all-reduce.2.cloned.1.call-start
  8906.8 73.6 all-reduce.2.cloned.1.call-start
  8983.7 73.6 all-reduce.2.cloned.1.call-start
  9060.6 73.5 all-reduce.2.cloned.1.call-start
  9231.5 73.6 all-reduce.2.cloned.1.call-start
  9385.0 73.6 all-reduce.2.cloned.1.call-start
  9708.8 73.6 all-reduce.2.cloned.1.call-start
  9879.4 73.6 all-reduce.2.cloned.1.call-start
  9956.3 73.6 all-reduce.2.cloned.1.call-start
  10203.5 73.6 all-reduce.2.cloned.1.call-start
  10280.5 73.3 all-reduce.2.cloned.1.call-start
  10357.1 73.6 all-reduce.2.cloned.1.call-start
  (65 other events, 4668.7 us)
Sparse Core Ops, SparseCore 0:
  159.8 69.3 all-reduce.1
  236.7 69.3 all-reduce.1
  483.6 69.3 all-reduce.1
  808.1 69.3 all-reduce.1
  885.0 69.3 all-reduce.1
  961.5 69.3 all-reduce.1
  1132.2 69.3 all-reduce.1
  1208.8 69.3 all-reduce.1
  1285.4 69.3 all-reduce.1
  1455.7 69.3 all-reduce.1
  1780.1 69.3 all-reduce.1
  1857.0 69.3 all-reduce.1
  2104.2 69.3 all-reduce.1
  2257.7 69.3 all-reduce.1
  2428.3 69.3 all-reduce.1
  2505.2 69.3 all-reduce.1
  2752.7 69.3 all-reduce.1
  3076.8 69.3 all-reduce.1
  3153.4 69.3 all-reduce.1
  3401.2 69.3 all-reduce.1
  3477.8 69.3 all-reduce.1
  3554.7 69.3 all-reduce.1
  3801.6 69.3 all-reduce.1
  3878.2 69.3 all-reduce.1
  4048.9 69.3 all-reduce.1
  4202.4 69.3 all-reduce.1
  4373.0 69.3 all-reduce.1
  4697.4 69.3 all-reduce.1
  4774.0 69.3 all-reduce.1
  5021.8 69.3 all-reduce.1
  5098.4 69.3 all-reduce.1
  5345.6 69.3 all-reduce.1
  5422.2 69.3 all-reduce.1
  5669.8 69.3 all-reduce.1
  5823.2 69.3 all-reduce.1
  6147.0 69.3 all-reduce.1
  6471.7 69.3 all-reduce.1
  6642.3 69.3 all-reduce.1
  6719.2 69.3 all-reduce.1
  6795.8 69.3 all-reduce.1
  6966.5 69.3 all-reduce.1
  7043.1 69.3 all-reduce.1
  7119.7 69.3 all-reduce.1
  7290.6 69.3 all-reduce.1
  7367.5 69.3 all-reduce.1
  7614.7 69.3 all-reduce.1
  7691.6 69.3 all-reduce.1
  7768.5 69.3 all-reduce.1
  8015.4 69.3 all-reduce.1
  8263.0 69.3 all-reduce.1
  8339.6 69.3 all-reduce.1
  8416.2 69.3 all-reduce.1
  8586.8 69.3 all-reduce.1
  8740.3 69.3 all-reduce.1
  8910.9 69.3 all-reduce.1
  9235.7 69.3 all-reduce.1
  9389.1 69.3 all-reduce.1
  9636.0 69.3 all-reduce.1
  9712.9 69.3 all-reduce.1
  9883.6 69.3 all-reduce.1
  9960.5 69.3 all-reduce.1
  10037.1 69.3 all-reduce.1
  10207.7 69.3 all-reduce.1
  10284.3 69.3 all-reduce.1
  (64 shorter events, 4361.8 us)
where the time goes:
time: 10500 us
  waiting for transfers between devices  9110 us (87%)
  matrix products  675 us (6%)
  blocking collectives  619 us (6%)
    psum x128, waiting for transfers between devices, inner_step(): w_sum = lax.psum(w_part, 'row')  9060 us
    all_gather x32, blocking collectives, outer_step(): v_all = lax.all_gather(v_own, 'col')  324 us
    dot_general x128, matrix products, inner_step(): jnp.dot(v_blk, y_blk, precision=FULL_PREC, preferred_element_type=jnp.flo...  274 us
    dot_general x128, matrix products, inner_step(): lax.dot_general(v_blk, x_in, CONTRACT_ROWS, precision=FULL_PREC, preferre...  253 us
    all_gather x32, blocking collectives, outer_step(): t_all = lax.all_gather(t_own, 'col')  242 us
  transfers between devices with their start and end apart: 129, of which 129 were waited for; matrix products, arithmetic and copies ran while one was open for 0% of the time, Pallas kernels for 0%

commit v1 on v0

v1 whole, which is shorter than its diff:
```python
import functools
import jax
import jax.numpy as jnp
from jax import lax
from jax.experimental import pallas as pl
from jax.experimental.pallas import tpu as pltpu
from jax.sharding import PartitionSpec as P

F32 = jnp.float32
BF16 = jnp.bfloat16
HI = lax.Precision.HIGHEST
GROUPS = ((1, 4), (5, 6), (7, 8), (9, 10), (11, 12), (13, 14), (15, 15), (16, 16))


def split3(v):
    h = v.astype(BF16)
    r = v - h.astype(F32)
    m = r.astype(BF16)
    l = (r - m.astype(F32)).astype(BF16)
    return h, m, l


def bdot(a, b):
    return jnp.dot(a, b, preferred_element_type=F32)


def fdot(a, b):
    return jnp.dot(a, b, precision=HI, preferred_element_type=F32)


def group_kernel(n_lo, n_hi, ag_ref, t_ref, x_in, x_ref, vin, tin, vh_s, vm_s, vl_s, gp_s, a_s, q_s, sem, tsem):
    def off(n):
        return pl.multiple_of(8 * (n * (n - 1) - n_lo * (n_lo - 1)), 16)

    def fetch(n, slot):
        base = off(n)

        def one(k, _):
            pltpu.make_async_copy(ag_ref.at[:, pl.ds(base + 16 * k, 16), :], vin.at[slot, k], sem.at[slot]).start()
            return 0

        lax.fori_loop(0, n, one, 0)
        pltpu.make_async_copy(t_ref.at[:, pl.ds(pl.multiple_of(64 * (16 - n), 64), 64), :], tin.at[slot], tsem.at[slot]).start()

    def arrive(n, slot):
        def one(k, _):
            pltpu.make_async_copy(ag_ref.at[:, pl.ds(0, 16), :], vin.at[slot, k], sem.at[slot]).wait()
            return 0

        lax.fori_loop(0, n, one, 0)
        pltpu.make_async_copy(t_ref.at[:, pl.ds(0, 64), :], tin.at[slot], tsem.at[slot]).wait()

    fetch(jnp.int32(n_lo), jnp.int32(0))
    x_ref[...] = x_in[...]

    ia = lax.broadcasted_iota(jnp.int32, (256, 256), 0) // 32
    ib = lax.broadcasted_iota(jnp.int32, (256, 256), 1) // 32

    def superblock(n, _):
        slot = lax.rem(n - n_lo, 2)
        arrive(n, slot)

        @pl.when(n < n_hi)
        def _():
            fetch(n + 1, 1 - slot)

        b = 16 - n
        gp_s[...] = jnp.zeros_like(gp_s)
        a_s[...] = jnp.zeros_like(a_s)
        q_s[...] = jnp.zeros_like(q_s)
        low = lax.broadcasted_iota(jnp.int32, (8, 16, 128), 2) < 64

        def gram(k, _):
            blk = vin[slot, k].reshape(8, 4, 16, 128)
            p = [blk[:, c] for c in range(4)]
            s = [pltpu.roll(q.reshape(128, 128), 64, 1).reshape(8, 16, 128) for q in p]
            top = jnp.concatenate([jnp.where(low, p[0], s[1]), jnp.where(low, p[2], s[3])], axis=2)
            bot = jnp.concatenate([jnp.where(low, s[0], p[1]), jnp.where(low, s[2], p[3])], axis=2)
            v = jnp.concatenate([top, bot], axis=1).reshape(256, 256)
            vh, vm, vl = split3(v)
            rows = pl.ds(pl.multiple_of(k * 256, 256), 256)
            vh_s[rows, :] = vh
            vm_s[rows, :] = vm
            vl_s[rows, :] = vl
            th, tm, tl = split3(v.T)
            x = x_ref[pl.ds(pl.multiple_of((b + k) * 256, 256), 256), :]
            xh, xm, xl = split3(x)
            x2 = jnp.concatenate([xh, xm], axis=1)
            gp_s[...] += bdot(
                jnp.concatenate([th, tm], axis=1),
                jnp.concatenate([jnp.concatenate([vh, x2], axis=1), jnp.concatenate([vm, x2], axis=1)], axis=0),
            )
            a_s[...] += bdot(jnp.concatenate([th, th], axis=1), jnp.concatenate([vm, vl], axis=0))
            q_s[...] += bdot(jnp.concatenate([tl, th], axis=1), jnp.concatenate([xh, xl], axis=0))
            return 0

        lax.fori_loop(0, n, gram, 0)

        a = a_s[...]
        g = gp_s[:, :256] + (a + a.T)
        w = (q_s[...] + gp_s[:, 384:]) + gp_s[:, 256:384]
        na = 4 * (ia % 2) + ia // 2
        nb = 4 * (ib % 2) + ib // 2
        t4 = tin[slot].reshape(256, 128)
        t = jnp.where(ia == ib, jnp.concatenate([t4, t4], axis=1), 0.0)
        for lev in (1, 2, 4):
            pick = (na // (2 * lev) == nb // (2 * lev)) & ((na // lev) % 2 == 0) & ((nb // lev) % 2 == 1)
            t = t - fdot(fdot(t, jnp.where(pick, g, 0.0)), t)
        yh, ym, yl = split3(fdot(t, w))
        y2 = jnp.concatenate([yh, ym], axis=1)
        y22 = jnp.concatenate([y2, y2], axis=0)
        yq = jnp.concatenate([yh, yl], axis=0)

        def update(k, _):
            rows = pl.ds(pl.multiple_of(k * 256, 256), 256)
            vh = vh_s[rows, :]
            z2 = bdot(jnp.concatenate([vh, vm_s[rows, :]], axis=1), y22)
            zq = bdot(jnp.concatenate([vl_s[rows, :], vh], axis=1), yq)
            xr = pl.ds(pl.multiple_of((b + k) * 256, 256), 256)
            x_ref[xr, :] = x_ref[xr, :] - ((zq + z2[:, 128:]) + z2[:, :128])
            return 0

        lax.fori_loop(0, n, update, 0)
        return 0

    lax.fori_loop(n_lo, n_hi + 1, superblock, 0)


def run_group(n_lo, n_hi, ag, t_all, x, interpret=False):
    return pl.pallas_call(
        functools.partial(group_kernel, n_lo, n_hi),
        out_shape=jax.ShapeDtypeStruct((4096, 128), F32),
        in_specs=[pl.BlockSpec(memory_space=pl.ANY), pl.BlockSpec(memory_space=pl.ANY), pl.BlockSpec(memory_space=pltpu.VMEM)],
        out_specs=pl.BlockSpec(memory_space=pltpu.VMEM),
        scratch_shapes=[
            pltpu.VMEM((2, 16, 32, 16, 128), F32),
            pltpu.VMEM((2, 4, 64, 128), F32),
            pltpu.VMEM((4096, 256), BF16),
            pltpu.VMEM((4096, 256), BF16),
            pltpu.VMEM((4096, 256), BF16),
            pltpu.VMEM((256, 512), F32),
            pltpu.VMEM((256, 256), F32),
            pltpu.VMEM((256, 128), F32),
            pltpu.SemaphoreType.DMA((2,)),
            pltpu.SemaphoreType.DMA((2,)),
        ],
        compiler_params=pltpu.CompilerParams(vmem_limit_bytes=48 * 1024 * 1024),
        cost_estimate=pl.CostEstimate(flops=sum(range(n_lo, n_hi + 1)) * 6 * 2 * 256 * 256 * 700, bytes_accessed=8 << 20, transcendentals=0),
        name=f"apply_{n_lo}_{n_hi}",
        interpret=interpret,
    )(ag, t_all, x)


def pack_piece(v_loc, n):
    b = 16 - n
    piece = v_loc[32 * b :, 64 * b : 64 * b + 64]
    return piece.reshape(n, 2, 16, 64).transpose(0, 2, 1, 3).reshape(16 * n, 128)


def solution(mesh):
    def local_apply(v_loc, t_loc, z_loc):
        t4 = jnp.tile(t_loc.reshape(1024, 32), (1, 4))
        t_all = lax.all_gather(t4, "col")
        gathered = []
        for n_lo, n_hi in GROUPS:
            piece = jnp.concatenate([pack_piece(v_loc, n) for n in range(n_lo, n_hi + 1)], axis=0)
            gathered.append(lax.all_gather(piece, ("row", "col")))
        x = z_loc.reshape(8, 16, 32, 128).transpose(1, 0, 2, 3).reshape(4096, 128)
        for (n_lo, n_hi), ag in zip(GROUPS, gathered):
            x = run_group(n_lo, n_hi, ag, t_all, x)
        return x.reshape(16, 8, 32, 128).transpose(1, 0, 2, 3).reshape(4096, 128)

    return jax.shard_map(
        local_apply,
        mesh=mesh,
        in_specs=(P("row", "col"), P("col", None, None), P(None, ("row", "col"))),
        out_specs=P(None, ("row", "col")),
        check_vma=False,
    )
```

time: 10500 us -> 585 us (0.06)
  waiting for transfers between devices: 9110 us -> 333 us
  matrix products: 675 us -> 0 us
  blocking collectives: 619 us -> 0 us
  Pallas kernels: 0 us -> 207 us
    psum x128 -> x0, waiting for transfers between devices: 9060 us -> none  [inner_step(): w_sum = lax.psum(w_part, 'row')]
    dot_general x384 -> x0, matrix products: 675 us -> none  [the longest x128 274 us: inner_step(): jnp.dot(v_blk, y_blk, precision=FULL_PREC, preferred_element_type=jnp.flo...]
    all_gather x64 -> x0, blocking collectives: 567 us -> none  [the longest x32 324 us: outer_step(): v_all = lax.all_gather(v_own, 'col')]
    all_gather x0 -> x9, waiting for transfers between devices: none -> 332 us  [the longest x8 322 us: local_apply(): gathered.append(lax.all_gather(piece, ('row', 'col')))]
    pallas_call x0 -> x8, Pallas kernels: none -> 207 us  [run_group(): pl.pallas_call(functools.partial(group_kernel, n_lo, n_hi), out_shape=jax...]
  transfers between devices with their start and end apart: 129 -> 9, of which waited for: 129 -> 9; matrix products, arithmetic and copies ran while one was open for 0% -> 2% of each run, Pallas kernels for 0% -> 32%
where the time goes in v1:
time: 585 us; the launch traced here: 581 us
  waiting for transfers between devices  333 us (57%)
  Pallas kernels  207 us (35%)
  local copies, waits for them, and re-layouts  23.5 us (4%)
  between operations  13.6 us (2%)
    all_gather x8, waiting for transfers between devices, local_apply(): gathered.append(lax.all_gather(piece, ('row', 'col')))  322 us
    pallas_call x8, Pallas kernels, run_group(): pl.pallas_call(functools.partial(group_kernel, n_lo, n_hi), out_shape=jax...  207 us
  transfers between devices with their start and end apart: 9, of which 9 were waited for; matrix products, arithmetic and copies ran while one was open for 2% of the time, Pallas kernels for 32%

profile of v1, /device:TPU:17, one launch (start us, length us, event | category | flops | bytes accessed | tf_op | source)
XLA Modules:
  0.0 581.4 jit_solution(13936041058049729206)
XLA Ops:
  6.5 1.4 copy.43
  8.0 1.0 copy.44
  9.3 0.1 reshape.137
  9.4 0.1 reshape.135
  9.5 0.1 reshape.133
  9.7 0.6 pad_maximum_fusion.5
  10.5 0.1 slice.58
  10.6 0.1 reshape.129
  10.8 0.1 reshape.127
  10.9 0.6 pad_maximum_fusion.4
  11.6 0.1 slice.56
  11.8 0.1 reshape.125
  12.0 0.1 reshape.123
  12.1 0.6 pad_maximum_fusion.3
  12.9 0.1 slice.54
  13.0 0.1 copy.51
  13.1 0.1 reshape.121
  13.3 0.1 reshape.119
  13.4 0.7 pad_maximum_fusion.2
  14.2 0.1 slice.52
  14.3 0.1 copy.49
  14.4 0.2 reshape.117
  14.6 0.1 copy.48
  14.7 0.2 reshape.115
  14.8 0.7 pad_maximum_fusion.1
  15.6 0.1 slice.50
  15.8 0.1 copy.47
  15.9 0.2 reshape.113
  16.1 0.1 copy.46
  16.2 0.2 reshape.111
  16.4 0.7 pad_maximum_fusion
  17.1 0.1 slice.49
  17.3 0.1 copy.65
  17.4 0.8 all_gather_reshape.7
  18.3 0.2 all-gather.16.cloned.1.call-start
  18.5 0.1 copy.64
  18.7 0.8 all_gather_reshape.6
  19.5 3.2 copy.60
  22.7 10.3 %all-gather.18.cloned.1.call-done.t_ref = f32[4,1024,128]{2,1,0:T(8,128)} async-done(((f32[1,1024,128]{2,1,0:T(8,128)}), f32[4,1024,128]{2,1,0:T(8,128)}) %all-gather.18.cloned.1.call-update) | async-done | bytes 2097168 | tf_op jit(solution)/shard_map/all_gather | solution.py:163
  33.0 58.9 %all-gather.32.cloned.1.call-done = f32[5120,128]{1,0:T(8,128)} async-done(((f32[160,128]{1,0:T(8,128)}), f32[5120,128]{1,0:T(8,128)}) %all-gather.32.cloned.1.call-update) | async-done | bytes 2621456 | tf_op jit(solution)/shard_map/all_gather | solution.py:167
  91.9 1.6 copy-done
  93.5 26.6 %apply_1_4.1.x_in = f32[4096,128]{1,0:T(8,128)S(1)} custom-call(f32[32,160,128]{2,1,0:T(8,128)} %bitcast.94, f32[4,1024,128]{2,1,0:T(8,128)S(1)} %copy-done, f32[4096,128]{1,0:T(8,128)} %bitcast.70), custom_call_target="tpu_custom_call" | custom-call | flops 5505024000 | bytes 8388608 | tf_op jit(solution)/shard_map/apply_1_4/pallas_call | solution.py:130
  120.1 1.3 copy-done.2
  121.5 30.6 %all-gather.30.cloned.1.call-done = f32[5632,128]{1,0:T(8,128)} async-done(((f32[176,128]{1,0:T(8,128)}), f32[5632,128]{1,0:T(8,128)}) %all-gather.30.cloned.1.call-update) | async-done | bytes 2883600 | tf_op jit(solution)/shard_map/all_gather | solution.py:167
  152.1 20.2 %apply_5_6.1.x_in = f32[4096,128]{1,0:T(8,128)S(1)} custom-call(f32[32,176,128]{2,1,0:T(8,128)} %bitcast.93, f32[4,1024,128]{2,1,0:T(8,128)S(1)} %copy-done.1, f32[4096,128]{1,0:T(8,128)} %copy-done.2), custom_call_target="tpu_custom_call" | custom-call | flops 6055526400 | bytes 8388608 | tf_op jit(solution)/shard_map/apply_5_6/pallas_call | solution.py:130
  172.2 1.3 copy-done.3
  173.6 41.6 %all-gather.28.cloned.1.call-done = f32[7680,128]{1,0:T(8,128)} async-done(((f32[240,128]{1,0:T(8,128)}), f32[7680,128]{1,0:T(8,128)}) %all-gather.28.cloned.1.call-update) | async-done | bytes 3932176 | tf_op jit(solution)/shard_map/all_gather | solution.py:167
  215.2 23.9 %apply_7_8.1.x_in = f32[4096,128]{1,0:T(8,128)S(1)} custom-call(f32[32,240,128]{2,1,0:T(8,128)} %bitcast.92, f32[4,1024,128]{2,1,0:T(8,128)S(1)} %copy-done.1, f32[4096,128]{1,0:T(8,128)} %copy-done.3), custom_call_target="tpu_custom_call" | custom-call | flops 8257536000 | bytes 8388608 | tf_op jit(solution)/shard_map/apply_7_8/pallas_call | solution.py:130
  239.1 1.3 copy-done.5
  240.4 41.1 %all-gather.26.cloned.1.call-done = f32[9728,128]{1,0:T(8,128)} async-done(((f32[304,128]{1,0:T(8,128)}), f32[9728,128]{1,0:T(8,128)}) %all-gather.26.cloned.1.call-update) | async-done | bytes 4980752 | tf_op jit(solution)/shard_map/all_gather | solution.py:167
  281.6 27.6 %apply_9_10.1.x_in = f32[4096,128]{1,0:T(8,128)S(1)} custom-call(f32[32,304,128]{2,1,0:T(8,128)} %bitcast.91, f32[4,1024,128]{2,1,0:T(8,128)S(1)} %copy-done.1, f32[4096,128]{1,0:T(8,128)} %copy-done.5), custom_call_target="tpu_custom_call" | custom-call | flops 10459545600 | bytes 8388608 | tf_op jit(solution)/shard_map/apply_9_10/pallas_call | solution.py:130
  309.2 1.3 copy-done.7
  310.5 41.1 %all-gather.24.cloned.1.call-done = f32[11776,128]{1,0:T(8,128)} async-done(((f32[368,128]{1,0:T(8,128)}), f32[11776,128]{1,0:T(8,128)}) %all-gather.24.cloned.1.call-update) | async-done | bytes 6029328 | tf_op jit(solution)/shard_map/all_gather | solution.py:167
  351.6 31.4 %apply_11_12.1.x_in = f32[4096,128]{1,0:T(8,128)S(1)} custom-call(f32[32,368,128]{2,1,0:T(8,128)} %bitcast.90, f32[4,1024,128]{2,1,0:T(8,128)S(1)} %copy-done.1, f32[4096,128]{1,0:T(8,128)} %copy-done.7), custom_call_target="tpu_custom_call" | custom-call | flops 12661555200 | bytes 8388608 | tf_op jit(solution)/shard_map/apply_11_12/pallas_call | solution.py:130
  383.0 1.3 copy-done.8
  384.3 41.3 %all-gather.22.cloned.1.call-done = f32[13824,128]{1,0:T(8,128)} async-done(((f32[432,128]{1,0:T(8,128)}), f32[13824,128]{1,0:T(8,128)}) %all-gather.22.cloned.1.call-update) | async-done | bytes 7077904 | tf_op jit(solution)/shard_map/all_gather | solution.py:167
  425.5 35.1 %apply_13_14.1.x_in = f32[4096,128]{1,0:T(8,128)S(1)} custom-call(f32[32,432,128]{2,1,0:T(8,128)} %bitcast.89, f32[4,1024,128]{2,1,0:T(8,128)S(1)} %copy-done.1, f32[4096,128]{1,0:T(8,128)} %copy-done.8), custom_call_target="tpu_custom_call" | custom-call | flops 14863564800 | bytes 8388608 | tf_op jit(solution)/shard_map/apply_13_14/pallas_call | solution.py:130
  460.7 1.3 copy-done.6
  462.0 25.9 %all-gather.20.cloned.1.call-done.ag_ref = f32[32,240,128]{2,1,0:T(8,128)} async-done(((f32[1,240,128]{2,1,0:T(8,128)}), f32[32,240,128]{2,1,0:T(8,128)}) %all-gather.20.cloned.1.call-update) | async-done | bytes 3932176 | tf_op jit(solution)/shard_map/all_gather | solution.py:167
  487.9 20.9 %apply_15_15.1.x_in = f32[4096,128]{1,0:T(8,128)S(1)} custom-call(f32[32,240,128]{2,1,0:T(8,128)} %all-gather.20.cloned.1.call-done.ag_ref, f32[4,1024,128]{2,1,0:T(8,128)S(1)} %copy-done.1, f32[4096,128]{1,0:T(8,128)} %copy-done.6), custom_call_target="tpu_custom_call" | custom-call | flops 8257536000 | bytes 8388608 | tf_op jit(solution)/shard_map/apply_15_15/pallas_call | solution.py:130
  508.8 1.3 copy-done.4
  510.2 41.6 %all-gather.16.cloned.1.call-done.ag_ref = f32[32,256,128]{2,1,0:T(8,128)} async-done(((f32[1,256,128]{2,1,0:T(8,128)}), f32[32,256,128]{2,1,0:T(8,128)}) %all-gather.16.cloned.1.call-update) | async-done | bytes 4194320 | tf_op jit(solution)/shard_map/all_gather | solution.py:167
  551.7 21.6 %apply_16_16.1 = f32[4096,128]{1,0:T(8,128)S(1)} custom-call(f32[32,256,128]{2,1,0:T(8,128)} %all-gather.16.cloned.1.call-done.ag_ref, f32[4,1024,128]{2,1,0:T(8,128)S(1)} %copy-done.1, f32[4096,128]{1,0:T(8,128)} %copy-done.4), custom_call_target="tpu_custom_call" | custom-call | flops 8808038400 | bytes 8388608 | tf_op jit(solution)/shard_map/apply_16_16/pallas_call | solution.py:130
  573.3 1.6 copy.61
  (51 shorter events, 1.3 us)
Async XLA Ops:
  6.5 2.5 copy-start.9
  6.5 26.4 %all-gather.18.cloned.1.call-start = ((), (), s32[]{:S(2)}) async-start(), calls=%async_computation.1 | async-start | bytes 2621440 | tf_op jit(solution)/shard_map/all_gather | solution.py:163
  9.0 82.9 %all-gather.32.cloned.1.call-start = ((), (), s32[]{:S(2)}) async-start(), calls=%async_computation.8 | async-start | bytes 2703360 | tf_op jit(solution)/shard_map/all_gather | solution.py:167
  10.4 141.7 %all-gather.30.cloned.1.call-start = ((), (), s32[]{:S(2)}) async-start(), calls=%async_computation.7 | async-start | bytes 2973696 | tf_op jit(solution)/shard_map/all_gather | solution.py:167
  11.5 203.7 %all-gather.28.cloned.1.call-start = ((), (), s32[]{:S(2)}) async-start(), calls=%async_computation.6 | async-start | bytes 4055040 | tf_op jit(solution)/shard_map/all_gather | solution.py:167
  12.8 268.8 %all-gather.26.cloned.1.call-start = ((), (), s32[]{:S(2)}) async-start(), calls=%async_computation.5 | async-start | bytes 5136384 | tf_op jit(solution)/shard_map/all_gather | solution.py:167
  14.1 337.5 %all-gather.24.cloned.1.call-start = ((), (), s32[]{:S(2)}) async-start(), calls=%async_computation.4 | async-start | bytes 6217728 | tf_op jit(solution)/shard_map/all_gather | solution.py:167
  15.5 410.0 %all-gather.22.cloned.1.call-start = ((), (), s32[]{:S(2)}) async-start(), calls=%async_computation.3 | async-start | bytes 7299072 | tf_op jit(solution)/shard_map/all_gather | solution.py:167
  15.8 2.7 slice-start
  17.1 470.8 %all-gather.20.cloned.1.call-start = ((), (), s32[]{:S(2)}) async-start(), calls=%async_computation.2 | async-start | bytes 4055040 | tf_op jit(solution)/shard_map/all_gather | solution.py:167
  18.3 533.4 %all-gather.16.cloned.1.call-start = ((), (), s32[]{:S(2)}) async-start(), calls=%async_computation | async-start | bytes 4325376 | tf_op jit(solution)/shard_map/all_gather | solution.py:167
  91.9 1.6 copy-start
  93.5 58.6 %copy-start.1 = (f32[4,1024,128]{2,1,0:T(8,128)S(1)}, f32[4,1024,128]{2,1,0:T(8,128)}, u32[]{:S(2)}) copy-start(f32[4,1024,128]{2,1,0:T(8,128)} %all-gather.18.cloned.1.call-done.t_ref) | copy-start | bytes 6291460
  120.1 1.3 copy-start.2
  172.2 1.3 copy-start.3
  239.1 1.3 copy-start.5
  309.2 1.3 copy-start.7
  383.0 1.3 copy-start.8
  460.7 1.3 copy-start.6
  508.8 1.3 copy-start.4
Sparse Core Ops, SparseCore 0:
  9.1 23.7 all-gather.17
  35.8 56.0 all-gather.31
  94.8 57.2 all-gather.29
  154.8 60.3 all-gather.27
  217.9 63.6 all-gather.25
  284.3 67.2 all-gather.23
  354.5 71.0 all-gather.21
  428.4 59.4 all-gather.19
  490.8 60.8 all-gather.15

commit v2 on v0

v2 whole, which is shorter than its diff:
```python
import functools
import jax
import jax.numpy as jnp
from jax import lax
from jax.experimental import pallas as pl
from jax.experimental.pallas import tpu as pltpu
from jax.sharding import PartitionSpec as P

F32 = jnp.float32
BF16 = jnp.bfloat16
HI = lax.Precision.HIGHEST
MESH = pl.DeviceIdType.MESH
UNITS = 36
Z_AHEAD = 6
D1 = 2
D2 = 2
LEAD = 0
LAG = D1 + D2


def split3(v):
    h = v.astype(BF16)
    r = v - h.astype(F32)
    m = r.astype(BF16)
    l = (r - m.astype(F32)).astype(BF16)
    return h, m, l


def bdot(a, b):
    return jnp.dot(a, b, preferred_element_type=F32)


def fdot(a, b):
    return jnp.dot(a, b, precision=HI, preferred_element_type=F32)


def loop(lo, hi, body):
    def step(i, carry):
        body(i)
        return carry

    lax.fori_loop(lo, hi, step, 0)


def fused_kernel(
    v_ref, t_ref, z_ref, o_ref, buf, tbuf, xbuf, vh_s, vm_s, vl_s, gp_s, a_s, q_s,
    in_sem, send_sem, z_sem, x1_sem, y1_sem, x2_sem, y2_sem, p_sem, t_sem,
):
    row, col = lax.axis_index("row"), lax.axis_index("col")
    z, y = row // 2, lax.rem(row, 2)
    x, c = col // 2, lax.rem(col, 2)
    x_dev = (row, (1 - x) * 2 + c)
    y_dev = (z * 2 + 1 - y, col)
    p_dev = (row, x * 2 + 1 - c)
    z_devs = [(lax.rem(z + k, 4) * 2 + y, col) for k in (1, 2, 3)]

    def unit(q):
        return pl.ds(pl.multiple_of(64 * q, 64), 64)

    def remote(view, recv, dev, kind):
        return pltpu.make_async_remote_copy(
            src_ref=view, dst_ref=view, send_sem=send_sem.at[kind], recv_sem=recv, device_id=dev, device_id_type=MESH
        )

    def z_copy(q, k):
        return remote(buf.at[c, x, y, z, unit(q)], z_sem.at[q], z_devs[k], 0)

    def x1_copy(q):
        return remote(buf.at[c, x, y, :, unit(q)], x1_sem.at[q], x_dev, 1)

    def y1_copy(q):
        return remote(buf.at[c, x, y, :, unit(q)], y1_sem.at[q], y_dev, 2)

    def y2_copy(q):
        return remote(buf.at[c, 1 - x, y, 0:2, unit(q)], y2_sem.at[q], y_dev, 3)

    def x2_copy(q):
        return remote(buf.at[c, x, 1 - y, 2:4, unit(q)], x2_sem.at[q], x_dev, 4)

    def p_copy(q, xx, yy):
        return remote(buf.at[c, xx, yy, :, unit(q)], p_sem.at[q], p_dev, 5)

    def z_land(q):
        return remote(buf.at[c, x, y, 0:3, unit(q)], z_sem.at[q], x_dev, 0)

    def x1_land(q):
        return remote(buf.at[c, 1 - x, y, :, unit(q)], x1_sem.at[q], x_dev, 1)

    def y1_land(q):
        return remote(buf.at[c, x, 1 - y, :, unit(q)], y1_sem.at[q], y_dev, 2)

    def y2_land(q):
        return remote(buf.at[c, 1 - x, 1 - y, 0:2, unit(q)], y2_sem.at[q], y_dev, 3)

    def x2_land(q):
        return remote(buf.at[c, 1 - x, 1 - y, 2:4, unit(q)], x2_sem.at[q], x_dev, 4)

    def p_land(q):
        return remote(buf.at[1 - c, :, :, :, unit(q)], p_sem.at[q], p_dev, 5)

    def z_send(q):
        for k in range(3):
            z_copy(q, k).start()

    def comm(q):
        @pl.when(q + Z_AHEAD < UNITS)
        def _():
            z_send(q + Z_AHEAD)

        @pl.when(q < UNITS)
        def _():
            z_land(q).wait_recv()
            x1_copy(q).start()
            y1_copy(q).start()
            p_copy(q, x, y).start()

        q1 = q - D1

        @pl.when((q1 >= 0) & (q1 < UNITS))
        def _():
            x1_land(q1).wait_recv()
            y2_copy(q1).start()
            y1_land(q1).wait_recv()
            x2_copy(q1).start()
            p_copy(q1, 1 - x, y).start()
            p_copy(q1, x, 1 - y).start()

        q2 = q - LAG

        @pl.when((q2 >= 0) & (q2 < UNITS))
        def _():
            y2_land(q2).wait_recv()
            x2_land(q2).wait_recv()
            p_copy(q2, 1 - x, 1 - y).start()

    def first_unit(n):
        return n * (n - 1) // 2

    def v_in(n, j):
        src = v_ref.at[pl.ds(pl.multiple_of(64 * (8 - n + j), 64), 64), pl.ds(pl.multiple_of(128 * (8 - n), 128), 128)]
        return pltpu.make_async_copy(src, buf.at[c, x, y, z, unit(first_unit(n) + j)], in_sem.at[0])

    def z_in(r):
        return pltpu.make_async_copy(z_ref.at[r], xbuf.at[:, lax.rem(r, 2), r // 2], in_sem.at[1])

    t_in = pltpu.make_async_copy(t_ref, tbuf.at[c, x], in_sem.at[2])
    loop(1, 9, lambda n: loop(0, n, lambda j: v_in(n, j).start()))
    t_in.start()
    loop(0, 8, lambda r: z_in(r).start())

    barrier = pltpu.get_barrier_semaphore()
    for dev in [x_dev, y_dev, p_dev] + z_devs:
        pl.semaphore_signal(barrier, inc=1, device_id=dev, device_id_type=MESH)
    own = buf.at[c, x, y, z]
    pltpu.make_async_copy(own, own, in_sem.at[0]).wait()
    pl.semaphore_wait(barrier, 6)

    loop(0, Z_AHEAD, z_send)
    t_in.wait()
    t_x = remote(tbuf.at[c, x], t_sem.at[0], x_dev, 6)
    t_p = [remote(tbuf.at[c, x], t_sem.at[1], p_dev, 7), remote(tbuf.at[c, 1 - x], t_sem.at[2], p_dev, 8)]
    t_x.start()
    t_p[0].start()
    loop(0, 1 + LAG + LEAD, comm)
    remote(tbuf.at[c, 1 - x], t_sem.at[0], x_dev, 6).wait_recv()
    t_p[1].start()
    pltpu.make_async_copy(xbuf, xbuf, in_sem.at[1]).wait()
    remote(tbuf.at[1 - c, x], t_sem.at[1], p_dev, 7).wait_recv()
    remote(tbuf.at[1 - c, 1 - x], t_sem.at[2], p_dev, 8).wait_recv()

    ia = lax.broadcasted_iota(jnp.int32, (256, 256), 0) // 32
    ib = lax.broadcasted_iota(jnp.int32, (256, 256), 1) // 32
    low = lax.broadcasted_iota(jnp.int32, (512, 128), 1) // 64

    def superblock(s):
        n = s // 2 + 1
        second = lax.rem(s, 2)
        h = 1 - second
        base = first_unit(n)

        @pl.when(second == 0)
        def _():
            loop(0, n, lambda j: p_land(base + j).wait_recv())

        gp_s[...] = jnp.zeros_like(gp_s)
        a_s[...] = jnp.zeros_like(a_s)
        q_s[...] = jnp.zeros_like(q_s)
        keep = low == h
        done = base + n + LAG + LEAD

        def gram(j):
            at = second * n + j

            @pl.when(n < 8)
            def _():
                loop(done + at * (n + 1) // (2 * n), done + (at + 1) * (n + 1) // (2 * n), comm)

            cols = []
            for xx in (0, 1):
                same = buf[h, xx, :, :, unit(base + j), :].reshape(512, 128)
                other = buf[1 - h, xx, :, :, unit(base + j), :].reshape(512, 128)
                cols.append(jnp.where(keep, same, pltpu.roll(other, 64, 1)))
            v = jnp.concatenate(cols, axis=1)
            vh, vm, vl = split3(v)
            rows = pl.ds(pl.multiple_of(j * 512, 512), 512)
            vh_s[rows, :] = vh
            vm_s[rows, :] = vm
            vl_s[rows, :] = vl
            th, tm, tl = split3(v.T)
            xh, xm, xl = split3(xbuf[8 - n + j].reshape(512, 128))
            x2 = jnp.concatenate([xh, xm], axis=1)
            gp_s[...] += bdot(
                jnp.concatenate([th, tm], axis=1),
                jnp.concatenate([jnp.concatenate([vh, x2], axis=1), jnp.concatenate([vm, x2], axis=1)], axis=0),
            )
            a_s[...] += bdot(jnp.concatenate([th, th], axis=1), jnp.concatenate([vm, vl], axis=0))
            q_s[...] += bdot(jnp.concatenate([tl, th], axis=1), jnp.concatenate([xh, xl], axis=0))

        loop(0, n, gram)

        a = a_s[...]
        g = gp_s[:, :256] + (a + a.T)
        w = (q_s[...] + gp_s[:, 384:]) + gp_s[:, 256:384]
        na = 4 * (ia % 2) + ia // 2
        nb = 4 * (ib % 2) + ib // 2
        diag = []
        t_rows = pl.ds(pl.multiple_of(32 * (8 - n), 32), 32)
        for xx in (0, 1):
            for cc in (0, 1):
                raw = tbuf[cc, xx, t_rows, :]
                e = jnp.where(h == cc, raw, pltpu.roll(raw, 64, 1))
                diag += [e, e]
        t4 = jnp.concatenate(diag, axis=0)
        t = jnp.where(ia == ib, jnp.concatenate([t4, t4], axis=1), 0.0)
        for lev in (1, 2, 4):
            pick = (na // (2 * lev) == nb // (2 * lev)) & ((na // lev) % 2 == 0) & ((nb // lev) % 2 == 1)
            t = t - fdot(fdot(t, jnp.where(pick, g, 0.0)), t)
        yh, ym, yl = split3(fdot(t, w))
        y2 = jnp.concatenate([yh, ym], axis=1)
        y22 = jnp.concatenate([y2, y2], axis=0)
        yq = jnp.concatenate([yh, yl], axis=0)

        def update(j):
            rows = pl.ds(pl.multiple_of(j * 512, 512), 512)
            vh = vh_s[rows, :]
            z2 = bdot(jnp.concatenate([vh, vm_s[rows, :]], axis=1), y22)
            zq = bdot(jnp.concatenate([vl_s[rows, :], vh], axis=1), yq)
            delta = (zq + z2[:, 128:]) + z2[:, :128]
            xbuf[8 - n + j] = xbuf[8 - n + j] - delta.reshape(2, 4, 64, 128)

        loop(0, n, update)

    loop(0, 16, superblock)

    def z_out(r):
        return pltpu.make_async_copy(xbuf.at[:, lax.rem(r, 2), r // 2], o_ref.at[r], in_sem.at[1])

    loop(0, 8, lambda r: z_out(r).start())

    remote(buf.at[c, x, y, 0:3], z_sem.at[0], x_dev, 0).wait_send()
    remote(buf.at[c, x, y], x1_sem.at[0], x_dev, 1).wait_send()
    remote(buf.at[c, x, y], y1_sem.at[0], y_dev, 2).wait_send()
    remote(buf.at[c, 1 - x, y, 0:2], y2_sem.at[0], y_dev, 3).wait_send()
    remote(buf.at[c, x, 1 - y, 2:4], x2_sem.at[0], x_dev, 4).wait_send()
    remote(buf.at[c], p_sem.at[0], p_dev, 5).wait_send()
    t_x.wait_send()
    t_p[0].wait_send()
    t_p[1].wait_send()
    pltpu.make_async_copy(xbuf, xbuf, in_sem.at[1]).wait()


def solution(mesh):
    def local_apply(v_loc, t_loc, z_loc):
        t2 = t_loc.reshape(8, 4, 32, 32).transpose(0, 2, 1, 3).reshape(256, 128)
        out = pl.pallas_call(
            fused_kernel,
            out_shape=jax.ShapeDtypeStruct((8, 8, 64, 128), F32),
            in_specs=[pl.BlockSpec(memory_space=pl.ANY)] * 3,
            out_specs=pl.BlockSpec(memory_space=pl.ANY),
            scratch_shapes=[
                pltpu.VMEM((2, 2, 2, 4, 64 * UNITS, 128), F32),
                pltpu.VMEM((2, 2, 256, 128), F32),
                pltpu.VMEM((8, 2, 4, 64, 128), F32),
                pltpu.VMEM((4096, 256), BF16),
                pltpu.VMEM((4096, 256), BF16),
                pltpu.VMEM((4096, 256), BF16),
                pltpu.VMEM((256, 512), F32),
                pltpu.VMEM((256, 256), F32),
                pltpu.VMEM((256, 128), F32),
                pltpu.SemaphoreType.DMA((3,)),
                pltpu.SemaphoreType.DMA((9,)),
                pltpu.SemaphoreType.DMA((UNITS,)),
                pltpu.SemaphoreType.DMA((UNITS,)),
                pltpu.SemaphoreType.DMA((UNITS,)),
                pltpu.SemaphoreType.DMA((UNITS,)),
                pltpu.SemaphoreType.DMA((UNITS,)),
                pltpu.SemaphoreType.DMA((UNITS,)),
                pltpu.SemaphoreType.DMA((3,)),
            ],
            compiler_params=pltpu.CompilerParams(
                collective_id=0, has_side_effects=True, vmem_limit_bytes=66 * 1000 * 1000
            ),
            name="gather_apply",
        )(v_loc, t2, z_loc.reshape(8, 8, 64, 128))
        return out.reshape(4096, 128)

    return jax.shard_map(
        local_apply,
        mesh=mesh,
        in_specs=(P("row", "col"), P("col", None, None), P(None, ("row", "col"))),
        out_specs=P(None, ("row", "col")),
        check_vma=False,
    )
```

time: 10500 us -> 230 us (0.02)
  the two profiles are of different devices: /device:TPU:17 before, /device:TPU:16 now
where the time goes in v2:
time: 230 us; the launch traced here: 229 us
  Pallas kernels  224 us (97%)
  local copies, waits for them, and re-layouts  5.34 us (2%)
    pallas_call x1, Pallas kernels, local_apply(): pl.pallas_call(fused_kernel, out_shape=jax.ShapeDtypeStruct((8, 8, 64, 12...  224 us

profile of v2, /device:TPU:16, one launch (start us, length us, event | category | flops | bytes accessed | tf_op | source)
XLA Modules:
  0.0 229.3 jit_solution(13228197996380876331)
XLA Ops:
  0.0 1.4 copy.6
  1.4 0.9 reshape.13.t_ref
  2.3 224.0 %gather_apply.1 = f32[8,8,64,128]{3,2,1,0:T(8,128)} custom-call(f32[512,1024]{1,0:T(8,128)} %v_ref.1, f32[256,128]{1,0:T(8,128)} %reshape.13.t_ref, f32[8,8,64,128]{3,2,1,0:T(8,128)} %bitcast.7), custom_call_target="tpu_custom_call" | custom-call | tf_op jit(solution)/shard_map/gather_apply/pallas_call | solution.py:275
  226.3 3.0 %copy.8 = f32[4096,128]{1,0:T(8,128)} copy(f32[4096,128]{1,0:T(8,128)} %bitcast.6) | data formatting | bytes 4194304

commit v3 on v2

--- a/solution.py
+++ b/solution.py
@@ -13,9 +13,9 @@
 UNITS = 36
 Z_AHEAD = 6
 D1 = 2
-D2 = 2
-LEAD = 0
-LAG = D1 + D2
+D2 = 1
+D3 = 1
+LAG = D1 + D2 + D3
 
 
 def split3(v):
@@ -44,7 +44,7 @@
 
 def fused_kernel(
     v_ref, t_ref, z_ref, o_ref, buf, tbuf, xbuf, vh_s, vm_s, vl_s, gp_s, a_s, q_s,
-    in_sem, send_sem, z_sem, x1_sem, y1_sem, x2_sem, y2_sem, p_sem, t_sem,
+    in_sem, send_sem, z_sem, x1_sem, y1_sem, x2_sem, y2_sem, z2_sem, p_sem, t_sem,
 ):
     row, col = lax.axis_index("row"), lax.axis_index("col")
     z, y = row // 2, lax.rem(row, 2)
@@ -52,6 +52,9 @@
     x_dev = (row, (1 - x) * 2 + c)
     y_dev = (z * 2 + 1 - y, col)
     p_dev = (row, x * 2 + 1 - c)
+    low_z = lax.rem(z, 2)
+    slot = 2 * low_z + z // 2
+    z2_dev = ((z + 1 - 2 * low_z) * 2 + y, col)
     z_devs = [(lax.rem(z + k, 4) * 2 + y, col) for k in (1, 2, 3)]
 
     def unit(q):
@@ -63,7 +66,7 @@
         )
 
     def z_copy(q, k):
-        return remote(buf.at[c, x, y, z, unit(q)], z_sem.at[q], z_devs[k], 0)
+        return remote(buf.at[c, x, y, slot, unit(q)], z_sem.at[q], z_devs[k], 0)
 
     def x1_copy(q):
         return remote(buf.at[c, x, y, :, unit(q)], x1_sem.at[q], x_dev, 1)
@@ -72,10 +75,13 @@
         return remote(buf.at[c, x, y, :, unit(q)], y1_sem.at[q], y_dev, 2)
 
     def y2_copy(q):
-        return remote(buf.at[c, 1 - x, y, 0:2, unit(q)], y2_sem.at[q], y_dev, 3)
+        return remote(buf.at[c, 1 - x, y, 2 * low_z, unit(q)], y2_sem.at[q], y_dev, 3)
 
     def x2_copy(q):
-        return remote(buf.at[c, x, 1 - y, 2:4, unit(q)], x2_sem.at[q], x_dev, 4)
+        return remote(buf.at[c, x, 1 - y, 2 * low_z + 1, unit(q)], x2_sem.at[q], x_dev, 4)
+
+    def z2_copy(q):
+        return remote(buf.at[c, 1 - x, 1 - y, pl.ds(2 * low_z, 2), unit(q)], z2_sem.at[q], z2_dev, 9)
 
     def p_copy(q, xx, yy):
         return remote(buf.at[c, xx, yy, :, unit(q)], p_sem.at[q], p_dev, 5)
@@ -90,10 +96,13 @@
         return remote(buf.at[c, x, 1 - y, :, unit(q)], y1_sem.at[q], y_dev, 2)
 
     def y2_land(q):
-        return remote(buf.at[c, 1 - x, 1 - y, 0:2, unit(q)], y2_sem.at[q], y_dev, 3)
+        return remote(buf.at[c, 1 - x, 1 - y, 2 * low_z, unit(q)], y2_sem.at[q], y_dev, 3)
 
     def x2_land(q):
-        return remote(buf.at[c, 1 - x, 1 - y, 2:4, unit(q)], x2_sem.at[q], x_dev, 4)
+        return remote(buf.at[c, 1 - x, 1 - y, 2 * low_z + 1, unit(q)], x2_sem.at[q], x_dev, 4)
+
+    def z2_land(q):
+        return remote(buf.at[c, 1 - x, 1 - y, pl.ds(2 - 2 * low_z, 2), unit(q)], z2_sem.at[q], z2_dev, 9)
 
     def p_land(q):
         return remote(buf.at[1 - c, :, :, :, unit(q)], p_sem.at[q], p_dev, 5)
@@ -125,23 +134,33 @@
             p_copy(q1, 1 - x, y).start()
             p_copy(q1, x, 1 - y).start()
 
-        q2 = q - LAG
+        q2 = q - D1 - D2
 
         @pl.when((q2 >= 0) & (q2 < UNITS))
         def _():
             y2_land(q2).wait_recv()
             x2_land(q2).wait_recv()
-            p_copy(q2, 1 - x, 1 - y).start()
+            z2_copy(q2).start()
+
+        q3 = q - LAG
+
+        @pl.when((q3 >= 0) & (q3 < UNITS))
+        def _():
+            z2_land(q3).wait_recv()
+            p_copy(q3, 1 - x, 1 - y).start()
 
     def first_unit(n):
         return n * (n - 1) // 2
 
     def v_in(n, j):
         src = v_ref.at[pl.ds(pl.multiple_of(64 * (8 - n + j), 64), 64), pl.ds(pl.multiple_of(128 * (8 - n), 128), 128)]
-        return pltpu.make_async_copy(src, buf.at[c, x, y, z, unit(first_unit(n) + j)], in_sem.at[0])
+        return pltpu.make_async_copy(src, buf.at[c, x, y, slot, unit(first_unit(n) + j)], in_sem.at[0])
+
+    def place(r):
+        return 2 * lax.rem(r // 2, 2) + r // 4
 
     def z_in(r):
-        return pltpu.make_async_copy(z_ref.at[r], xbuf.at[:, lax.rem(r, 2), r // 2], in_sem.at[1])
+        return pltpu.make_async_copy(z_ref.at[r], xbuf.at[:, lax.rem(r, 2), place(r)], in_sem.at[1])
 
     t_in = pltpu.make_async_copy(t_ref, tbuf.at[c, x], in_sem.at[2])
     loop(1, 9, lambda n: loop(0, n, lambda j: v_in(n, j).start()))
@@ -151,7 +170,7 @@
     barrier = pltpu.get_barrier_semaphore()
     for dev in [x_dev, y_dev, p_dev] + z_devs:
         pl.semaphore_signal(barrier, inc=1, device_id=dev, device_id_type=MESH)
-    own = buf.at[c, x, y, z]
+    own = buf.at[c, x, y, slot]
     pltpu.make_async_copy(own, own, in_sem.at[0]).wait()
     pl.semaphore_wait(barrier, 6)
 
@@ -161,7 +180,7 @@
     t_p = [remote(tbuf.at[c, x], t_sem.at[1], p_dev, 7), remote(tbuf.at[c, 1 - x], t_sem.at[2], p_dev, 8)]
     t_x.start()
     t_p[0].start()
-    loop(0, 1 + LAG + LEAD, comm)
+    loop(0, 1 + LAG, comm)
     remote(tbuf.at[c, 1 - x], t_sem.at[0], x_dev, 6).wait_recv()
     t_p[1].start()
     pltpu.make_async_copy(xbuf, xbuf, in_sem.at[1]).wait()
@@ -172,28 +191,36 @@
     ib = lax.broadcasted_iota(jnp.int32, (256, 256), 1) // 32
     low = lax.broadcasted_iota(jnp.int32, (512, 128), 1) // 64
 
+    def steps(n):
+        return first_unit(n) + LAG + n - (n - 1) // 2
+
     def superblock(s):
         n = s // 2 + 1
         second = lax.rem(s, 2)
         h = 1 - second
         base = first_unit(n)
 
-        @pl.when(second == 0)
-        def _():
-            loop(0, n, lambda j: p_land(base + j).wait_recv())
-
         gp_s[...] = jnp.zeros_like(gp_s)
         a_s[...] = jnp.zeros_like(a_s)
         q_s[...] = jnp.zeros_like(q_s)
         keep = low == h
-        done = base + n + LAG + LEAD
 
         def gram(j):
             at = second * n + j
 
             @pl.when(n < 8)
             def _():
-                loop(done + at * (n + 1) // (2 * n), done + (at + 1) * (n + 1) // (2 * n), comm)
+                grow = steps(n + 1) - steps(n)
+                loop(steps(n) + at * grow // (2 * n), steps(n) + (at + 1) * grow // (2 * n), comm)
+
+            @pl.when((n == 8) & (second == 0))
+            def _():
+                grow = UNITS + LAG - steps(8)
+                loop(steps(8) + j * grow // 8, steps(8) + (j + 1) * grow // 8, comm)
+
+            @pl.when(second == 0)
+            def _():
+                p_land(base + j).wait_recv()
 
             cols = []
             for xx in (0, 1):
@@ -253,15 +280,16 @@
     loop(0, 16, superblock)
 
     def z_out(r):
-        return pltpu.make_async_copy(xbuf.at[:, lax.rem(r, 2), r // 2], o_ref.at[r], in_sem.at[1])
+        return pltpu.make_async_copy(xbuf.at[:, lax.rem(r, 2), place(r)], o_ref.at[r], in_sem.at[1])
 
     loop(0, 8, lambda r: z_out(r).start())
 
     remote(buf.at[c, x, y, 0:3], z_sem.at[0], x_dev, 0).wait_send()
     remote(buf.at[c, x, y], x1_sem.at[0], x_dev, 1).wait_send()
     remote(buf.at[c, x, y], y1_sem.at[0], y_dev, 2).wait_send()
-    remote(buf.at[c, 1 - x, y, 0:2], y2_sem.at[0], y_dev, 3).wait_send()
-    remote(buf.at[c, x, 1 - y, 2:4], x2_sem.at[0], x_dev, 4).wait_send()
+    remote(buf.at[c, 1 - x, y, 0], y2_sem.at[0], y_dev, 3).wait_send()
+    remote(buf.at[c, x, 1 - y, 0], x2_sem.at[0], x_dev, 4).wait_send()
+    remote(buf.at[c, 1 - x, 1 - y, 0:2], z2_sem.at[0], z2_dev, 9).wait_send()
     remote(buf.at[c], p_sem.at[0], p_dev, 5).wait_send()
     t_x.wait_send()
     t_p[0].wait_send()
@@ -288,7 +316,8 @@
                 pltpu.VMEM((256, 256), F32),
                 pltpu.VMEM((256, 128), F32),
                 pltpu.SemaphoreType.DMA((3,)),
-                pltpu.SemaphoreType.DMA((9,)),
+                pltpu.SemaphoreType.DMA((10,)),
+                pltpu.SemaphoreType.DMA((UNITS,)),
                 pltpu.SemaphoreType.DMA((UNITS,)),
                 pltpu.SemaphoreType.DMA((UNITS,)),
                 pltpu.SemaphoreType.DMA((UNITS,)),

time: 230 us -> 264 us (1.15)
  the two profiles are of different devices: /device:TPU:16 before, /device:TPU:17 now
where the time goes in v3:
time: 264 us; the launch traced here: 263 us
  Pallas kernels  258 us (98%)
  local copies, waits for them, and re-layouts  5.34 us (2%)
    pallas_call x1, Pallas kernels, local_apply(): pl.pallas_call(fused_kernel, out_shape=jax.ShapeDtypeStruct((8, 8, 64, 12...  258 us

profile of v3, /device:TPU:17, one launch (start us, length us, event | category | flops | bytes accessed | tf_op | source)
XLA Modules:
  0.0 263.5 jit_solution(2885205479394543701)
XLA Ops:
  0.0 1.4 copy.6
  1.4 0.9 reshape.13.t_ref
  2.3 258.1 %gather_apply.1 = f32[8,8,64,128]{3,2,1,0:T(8,128)} custom-call(f32[512,1024]{1,0:T(8,128)} %v_ref.1, f32[256,128]{1,0:T(8,128)} %reshape.13.t_ref, f32[8,8,64,128]{3,2,1,0:T(8,128)} %bitcast.7), custom_call_target="tpu_custom_call" | custom-call | tf_op jit(solution)/shard_map/gather_apply/pallas_call | solution.py:303
  260.4 3.0 %copy.8 = f32[4096,128]{1,0:T(8,128)} copy(f32[4096,128]{1,0:T(8,128)} %bitcast.6) | data formatting | bytes 4194304

commit v4 on v3

--- a/solution.py
+++ b/solution.py
@@ -12,9 +12,9 @@
 MESH = pl.DeviceIdType.MESH
 UNITS = 36
 Z_AHEAD = 6
-D1 = 2
-D2 = 1
-D3 = 1
+D1 = 3
+D2 = 2
+D3 = 2
 LAG = D1 + D2 + D3
 
 
@@ -30,6 +30,10 @@
     return jnp.dot(a, b, preferred_element_type=F32)
 
 
+def ndot(a, b):
+    return lax.dot_general(a, b, (((1,), (1,)), ((), ())), preferred_element_type=F32)
+
+
 def fdot(a, b):
     return jnp.dot(a, b, precision=HI, preferred_element_type=F32)
 
@@ -43,8 +47,8 @@
 
 
 def fused_kernel(
-    v_ref, t_ref, z_ref, o_ref, buf, tbuf, xbuf, vh_s, vm_s, vl_s, gp_s, a_s, q_s,
-    in_sem, send_sem, z_sem, x1_sem, y1_sem, x2_sem, y2_sem, z2_sem, p_sem, t_sem,
+    v_ref, t_ref, z_ref, o_ref, buf, tbuf, stage, xt, tx, vh_s, vm_s, vl_s, g_s, a_s, w_s,
+    in_sem, send_sem, z_sem, x1_sem, y1_sem, x2_sem, y2_sem, z2_sem, p_sem, t_sem, tx_sem,
 ):
     row, col = lax.axis_index("row"), lax.axis_index("col")
     z, y = row // 2, lax.rem(row, 2)
@@ -116,13 +120,6 @@
         def _():
             z_send(q + Z_AHEAD)
 
-        @pl.when(q < UNITS)
-        def _():
-            z_land(q).wait_recv()
-            x1_copy(q).start()
-            y1_copy(q).start()
-            p_copy(q, x, y).start()
-
         q1 = q - D1
 
         @pl.when((q1 >= 0) & (q1 < UNITS))
@@ -134,6 +131,13 @@
             p_copy(q1, 1 - x, y).start()
             p_copy(q1, x, 1 - y).start()
 
+        @pl.when(q < UNITS)
+        def _():
+            z_land(q).wait_recv()
+            x1_copy(q).start()
+            y1_copy(q).start()
+            p_copy(q, x, y).start()
+
         q2 = q - D1 - D2
 
         @pl.when((q2 >= 0) & (q2 < UNITS))
@@ -160,7 +164,7 @@
         return 2 * lax.rem(r // 2, 2) + r // 4
 
     def z_in(r):
-        return pltpu.make_async_copy(z_ref.at[r], xbuf.at[:, lax.rem(r, 2), place(r)], in_sem.at[1])
+        return pltpu.make_async_copy(z_ref.at[r], stage.at[:, lax.rem(r, 2), place(r)], in_sem.at[1])
 
     t_in = pltpu.make_async_copy(t_ref, tbuf.at[c, x], in_sem.at[2])
     loop(1, 9, lambda n: loop(0, n, lambda j: v_in(n, j).start()))
@@ -183,7 +187,12 @@
     loop(0, 1 + LAG, comm)
     remote(tbuf.at[c, 1 - x], t_sem.at[0], x_dev, 6).wait_recv()
     t_p[1].start()
-    pltpu.make_async_copy(xbuf, xbuf, in_sem.at[1]).wait()
+    pltpu.make_async_copy(stage, stage, in_sem.at[1]).wait()
+
+    def turn_in(u):
+        xt[u] = stage[u].reshape(512, 128).T
+
+    loop(0, 8, turn_in)
     remote(tbuf.at[1 - c, x], t_sem.at[1], p_dev, 7).wait_recv()
     remote(tbuf.at[1 - c, 1 - x], t_sem.at[2], p_dev, 8).wait_recv()
 
@@ -192,62 +201,49 @@
     low = lax.broadcasted_iota(jnp.int32, (512, 128), 1) // 64
 
     def steps(n):
-        return first_unit(n) + LAG + n - (n - 1) // 2
-
-    def superblock(s):
-        n = s // 2 + 1
-        second = lax.rem(s, 2)
-        h = 1 - second
+        return first_unit(n) + LAG + n - n // 4
+
+    def share(n, at):
+        grow = steps(n + 1) - steps(n)
+        loop(steps(n) + at * grow // (3 * n), steps(n) + (at + 1) * grow // (3 * n), comm)
+
+    def assemble(q, h):
+        cols = []
+        for xx in (0, 1):
+            same = buf[h, xx, :, :, unit(q), :].reshape(512, 128)
+            other = buf[1 - h, xx, :, :, unit(q), :].reshape(512, 128)
+            cols.append(jnp.where(low == h, same, pltpu.roll(other, 64, 1)))
+        return jnp.concatenate(cols, axis=1)
+
+    def t_copy(n, half):
+        return remote(tx.at[n - 1, half], tx_sem.at[n - 1], p_dev, 10)
+
+    def pair(n):
         base = first_unit(n)
-
-        gp_s[...] = jnp.zeros_like(gp_s)
+        g_s[...] = jnp.zeros_like(g_s)
         a_s[...] = jnp.zeros_like(a_s)
-        q_s[...] = jnp.zeros_like(q_s)
-        keep = low == h
 
         def gram(j):
-            at = second * n + j
-
             @pl.when(n < 8)
             def _():
-                grow = steps(n + 1) - steps(n)
-                loop(steps(n) + at * grow // (2 * n), steps(n) + (at + 1) * grow // (2 * n), comm)
-
-            @pl.when((n == 8) & (second == 0))
+                share(n, j)
+
+            @pl.when(n == 8)
             def _():
                 grow = UNITS + LAG - steps(8)
                 loop(steps(8) + j * grow // 8, steps(8) + (j + 1) * grow // 8, comm)
 
-            @pl.when(second == 0)
-            def _():
-                p_land(base + j).wait_recv()
-
-            cols = []
-            for xx in (0, 1):
-                same = buf[h, xx, :, :, unit(base + j), :].reshape(512, 128)
-                other = buf[1 - h, xx, :, :, unit(base + j), :].reshape(512, 128)
-                cols.append(jnp.where(keep, same, pltpu.roll(other, 64, 1)))
-            v = jnp.concatenate(cols, axis=1)
+            p_land(base + j).wait_recv()
+            v = assemble(base + j, c)
             vh, vm, vl = split3(v)
-            rows = pl.ds(pl.multiple_of(j * 512, 512), 512)
-            vh_s[rows, :] = vh
-            vm_s[rows, :] = vm
-            vl_s[rows, :] = vl
-            th, tm, tl = split3(v.T)
-            xh, xm, xl = split3(xbuf[8 - n + j].reshape(512, 128))
-            x2 = jnp.concatenate([xh, xm], axis=1)
-            gp_s[...] += bdot(
-                jnp.concatenate([th, tm], axis=1),
-                jnp.concatenate([jnp.concatenate([vh, x2], axis=1), jnp.concatenate([vm, x2], axis=1)], axis=0),
-            )
+            th, tm, _ = split3(v.T)
+            g_s[...] += bdot(jnp.concatenate([th, tm], axis=1), jnp.concatenate([vh, vm], axis=0))
             a_s[...] += bdot(jnp.concatenate([th, th], axis=1), jnp.concatenate([vm, vl], axis=0))
-            q_s[...] += bdot(jnp.concatenate([tl, th], axis=1), jnp.concatenate([xh, xl], axis=0))
 
         loop(0, n, gram)
 
         a = a_s[...]
-        g = gp_s[:, :256] + (a + a.T)
-        w = (q_s[...] + gp_s[:, 384:]) + gp_s[:, 256:384]
+        g = g_s[...] + (a + a.T)
         na = 4 * (ia % 2) + ia // 2
         nb = 4 * (ib % 2) + ib // 2
         diag = []
@@ -255,34 +251,68 @@
         for xx in (0, 1):
             for cc in (0, 1):
                 raw = tbuf[cc, xx, t_rows, :]
-                e = jnp.where(h == cc, raw, pltpu.roll(raw, 64, 1))
+                e = jnp.where(c == cc, raw, pltpu.roll(raw, 64, 1))
                 diag += [e, e]
         t4 = jnp.concatenate(diag, axis=0)
         t = jnp.where(ia == ib, jnp.concatenate([t4, t4], axis=1), 0.0)
         for lev in (1, 2, 4):
             pick = (na // (2 * lev) == nb // (2 * lev)) & ((na // lev) % 2 == 0) & ((nb // lev) % 2 == 1)
             t = t - fdot(fdot(t, jnp.where(pick, g, 0.0)), t)
-        yh, ym, yl = split3(fdot(t, w))
-        y2 = jnp.concatenate([yh, ym], axis=1)
-        y22 = jnp.concatenate([y2, y2], axis=0)
-        yq = jnp.concatenate([yh, yl], axis=0)
-
-        def update(j):
-            rows = pl.ds(pl.multiple_of(j * 512, 512), 512)
-            vh = vh_s[rows, :]
-            z2 = bdot(jnp.concatenate([vh, vm_s[rows, :]], axis=1), y22)
-            zq = bdot(jnp.concatenate([vl_s[rows, :], vh], axis=1), yq)
-            delta = (zq + z2[:, 128:]) + z2[:, :128]
-            xbuf[8 - n + j] = xbuf[8 - n + j] - delta.reshape(2, 4, 64, 128)
-
-        loop(0, n, update)
-
-    loop(0, 16, superblock)
-
-    def z_out(r):
-        return pltpu.make_async_copy(xbuf.at[:, lax.rem(r, 2), place(r)], o_ref.at[r], in_sem.at[1])
-
-    loop(0, 8, lambda r: z_out(r).start())
+        tx[n - 1, c] = t.T
+        t_copy(n, c).start()
+
+        def half(second):
+            h = 1 - second
+            w_s[...] = jnp.zeros_like(w_s)
+
+            def project(j):
+                @pl.when(n < 8)
+                def _():
+                    share(n, (1 + second) * n + j)
+
+                vh, vm, vl = split3(assemble(base + j, h))
+                rows = pl.ds(pl.multiple_of(j * 512, 512), 512)
+                vh_s[rows, :] = vh
+                vm_s[rows, :] = vm
+                vl_s[rows, :] = vl
+                xh, xm, xl = split3(xt[8 - n + j])
+                p1 = bdot(jnp.concatenate([xh, xm, xl], axis=0), vh)
+                p2 = bdot(jnp.concatenate([xh, xm], axis=0), vm)
+                p3 = bdot(xh, vl)
+                w_s[...] += (((p3 + p1[256:]) + p2[128:]) + (p2[:128] + p1[128:256])) + p1[:128]
+
+            loop(0, n, project)
+
+            @pl.when(second == 0)
+            def _():
+                t_copy(n, 1 - c).wait_recv()
+
+            yh, ym, yl = split3(fdot(w_s[...], tx[n - 1, h]))
+            y2 = jnp.concatenate([yh, ym], axis=0)
+            y3 = jnp.concatenate([yh, ym, yl], axis=0)
+
+            def update(j):
+                rows = pl.ds(pl.multiple_of(j * 512, 512), 512)
+                d1 = ndot(y3, vh_s[rows, :])
+                d2 = ndot(y2, vm_s[rows, :])
+                d3 = ndot(yh, vl_s[rows, :])
+                xt[8 - n + j] -= (((d3 + d1[256:]) + d2[128:]) + (d2[:128] + d1[128:256])) + d1[:128]
+
+            loop(0, n, update)
+
+        loop(0, 2, half)
+
+    loop(1, 9, pair)
+
+    def turn_out(u):
+        stage[u] = xt[u].T.reshape(2, 4, 64, 128)
+
+        def z_out(r):
+            pltpu.make_async_copy(stage.at[u, lax.rem(r, 2), place(r)], o_ref.at[r, u], in_sem.at[1]).start()
+
+        loop(0, 8, z_out)
+
+    loop(0, 8, turn_out)
 
     remote(buf.at[c, x, y, 0:3], z_sem.at[0], x_dev, 0).wait_send()
     remote(buf.at[c, x, y], x1_sem.at[0], x_dev, 1).wait_send()
@@ -294,7 +324,8 @@
     t_x.wait_send()
     t_p[0].wait_send()
     t_p[1].wait_send()
-    pltpu.make_async_copy(xbuf, xbuf, in_sem.at[1]).wait()
+    remote(tx.at[:, 0], tx_sem.at[0], p_dev, 10).wait_send()
+    pltpu.make_async_copy(stage, stage, in_sem.at[1]).wait()
 
 
 def solution(mesh):
@@ -309,14 +340,16 @@
                 pltpu.VMEM((2, 2, 2, 4, 64 * UNITS, 128), F32),
                 pltpu.VMEM((2, 2, 256, 128), F32),
                 pltpu.VMEM((8, 2, 4, 64, 128), F32),
+                pltpu.VMEM((8, 128, 512), F32),
+                pltpu.VMEM((8, 2, 256, 256), F32),
                 pltpu.VMEM((4096, 256), BF16),
                 pltpu.VMEM((4096, 256), BF16),
                 pltpu.VMEM((4096, 256), BF16),
-                pltpu.VMEM((256, 512), F32),
                 pltpu.VMEM((256, 256), F32),
-                pltpu.VMEM((256, 128), F32),
+                pltpu.VMEM((256, 256), F32),
+                pltpu.VMEM((128, 256), F32),
                 pltpu.SemaphoreType.DMA((3,)),
-                pltpu.SemaphoreType.DMA((10,)),
+                pltpu.SemaphoreType.DMA((11,)),
                 pltpu.SemaphoreType.DMA((UNITS,)),
                 pltpu.SemaphoreType.DMA((UNITS,)),
                 pltpu.SemaphoreType.DMA((UNITS,)),
@@ -325,6 +358,7 @@
                 pltpu.SemaphoreType.DMA((UNITS,)),
                 pltpu.SemaphoreType.DMA((UNITS,)),
                 pltpu.SemaphoreType.DMA((3,)),
+                pltpu.SemaphoreType.DMA((8,)),
             ],
             compiler_params=pltpu.CompilerParams(
                 collective_id=0, has_side_effects=True, vmem_limit_bytes=66 * 1000 * 1000

time: 264 us -> 196 us (0.74)
  Pallas kernels: 258 us -> 191 us
    pallas_call x1, Pallas kernels: 258 us -> 191 us  [local_apply(): pl.pallas_call(fused_kernel, out_shape=jax.ShapeDtypeStruct((8, 8, 64, 12...]
where the time goes in v4:
time: 196 us
  Pallas kernels  191 us (97%)
  local copies, waits for them, and re-layouts  5.34 us (3%)
    pallas_call x1, Pallas kernels, local_apply(): pl.pallas_call(fused_kernel, out_shape=jax.ShapeDtypeStruct((8, 8, 64, 12...  191 us

profile of v4, /device:TPU:17, one launch (start us, length us, event | category | flops | bytes accessed | tf_op | source)
XLA Modules:
  0.0 196.0 jit_solution(18015061852894240212)
XLA Ops:
  0.0 1.4 copy.6
  1.4 0.9 reshape.13.t_ref
  2.3 190.7 %gather_apply.1 = f32[8,8,64,128]{3,2,1,0:T(8,128)} custom-call(f32[512,1024]{1,0:T(8,128)} %v_ref.1, f32[256,128]{1,0:T(8,128)} %reshape.13.t_ref, f32[8,8,64,128]{3,2,1,0:T(8,128)} %bitcast.7), custom_call_target="tpu_custom_call" | custom-call | tf_op jit(solution)/shard_map/gather_apply/pallas_call | solution.py:334
  193.0 3.0 %copy.8 = f32[4096,128]{1,0:T(8,128)} copy(f32[4096,128]{1,0:T(8,128)} %bitcast.6) | data formatting | bytes 4194304

commit v5 on v4

--- a/solution.py
+++ b/solution.py
@@ -12,9 +12,9 @@
 MESH = pl.DeviceIdType.MESH
 UNITS = 36
 Z_AHEAD = 6
-D1 = 3
-D2 = 2
-D3 = 2
+D1 = 2
+D2 = 1
+D3 = 1
 LAG = D1 + D2 + D3
 
 
@@ -47,7 +47,7 @@
 
 
 def fused_kernel(
-    v_ref, t_ref, z_ref, o_ref, buf, tbuf, stage, xt, tx, vh_s, vm_s, vl_s, g_s, a_s, w_s,
+    v_ref, t_ref, z_ref, o_ref, buf, traw, tbuf, stage, xt, tx, vh_s, vm_s, vl_s, g_s, a_s, w_s,
     in_sem, send_sem, z_sem, x1_sem, y1_sem, x2_sem, y2_sem, z2_sem, p_sem, t_sem, tx_sem,
 ):
     row, col = lax.axis_index("row"), lax.axis_index("col")
@@ -166,7 +166,7 @@
     def z_in(r):
         return pltpu.make_async_copy(z_ref.at[r], stage.at[:, lax.rem(r, 2), place(r)], in_sem.at[1])
 
-    t_in = pltpu.make_async_copy(t_ref, tbuf.at[c, x], in_sem.at[2])
+    t_in = pltpu.make_async_copy(t_ref, traw, in_sem.at[2])
     loop(1, 9, lambda n: loop(0, n, lambda j: v_in(n, j).start()))
     t_in.start()
     loop(0, 8, lambda r: z_in(r).start())
@@ -180,11 +180,18 @@
 
     loop(0, Z_AHEAD, z_send)
     t_in.wait()
+
+    def pack_t(b):
+        rows = pl.ds(pl.multiple_of(32 * b, 32), 32)
+        tbuf[c, x, rows, :] = jnp.concatenate([traw[4 * b + k] for k in range(4)], axis=1)
+
+    loop(0, 8, pack_t)
+    loop(0, 2, comm)
     t_x = remote(tbuf.at[c, x], t_sem.at[0], x_dev, 6)
     t_p = [remote(tbuf.at[c, x], t_sem.at[1], p_dev, 7), remote(tbuf.at[c, 1 - x], t_sem.at[2], p_dev, 8)]
     t_x.start()
     t_p[0].start()
-    loop(0, 1 + LAG, comm)
+    loop(2, 1 + LAG, comm)
     remote(tbuf.at[c, 1 - x], t_sem.at[0], x_dev, 6).wait_recv()
     t_p[1].start()
     pltpu.make_async_copy(stage, stage, in_sem.at[1]).wait()
@@ -201,11 +208,11 @@
     low = lax.broadcasted_iota(jnp.int32, (512, 128), 1) // 64
 
     def steps(n):
-        return first_unit(n) + LAG + n - n // 4
+        return first_unit(n) + LAG + n - n // 4 - 2 * (n // 8)
 
     def share(n, at):
         grow = steps(n + 1) - steps(n)
-        loop(steps(n) + at * grow // (3 * n), steps(n) + (at + 1) * grow // (3 * n), comm)
+        loop(steps(n) + at * grow // (4 * n), steps(n) + (at + 1) * grow // (4 * n), comm)
 
     def assemble(q, h):
         cols = []
@@ -222,6 +229,26 @@
         base = first_unit(n)
         g_s[...] = jnp.zeros_like(g_s)
         a_s[...] = jnp.zeros_like(a_s)
+        w_s[...] = jnp.zeros_like(w_s)
+
+        def apply_v(j, h):
+            vh, vm, vl = split3(assemble(base + j, h))
+            rows = pl.ds(pl.multiple_of(j * 512, 512), 512)
+            vh_s[rows, :] = vh
+            vm_s[rows, :] = vm
+            vl_s[rows, :] = vl
+            xh, xm, xl = split3(xt[8 - n + j])
+            p1 = bdot(jnp.concatenate([xh, xm, xl], axis=0), vh)
+            p2 = bdot(jnp.concatenate([xh, xm], axis=0), vm)
+            p3 = bdot(xh, vl)
+            w_s[...] += (((p3 + p1[256:]) + p2[128:]) + (p2[:128] + p1[128:256])) + p1[:128]
+
+        def project(j):
+            @pl.when(n < 8)
+            def _():
+                share(n, 2 * n + j)
+
+            apply_v(j, 0)
 
         def gram(j):
             @pl.when(n < 8)
@@ -239,6 +266,7 @@
             th, tm, _ = split3(v.T)
             g_s[...] += bdot(jnp.concatenate([th, tm], axis=1), jnp.concatenate([vh, vm], axis=0))
             a_s[...] += bdot(jnp.concatenate([th, th], axis=1), jnp.concatenate([vm, vl], axis=0))
+            apply_v(j, 1)
 
         loop(0, n, gram)
 
@@ -263,25 +291,11 @@
 
         def half(second):
             h = 1 - second
-            w_s[...] = jnp.zeros_like(w_s)
-
-            def project(j):
-                @pl.when(n < 8)
-                def _():
-                    share(n, (1 + second) * n + j)
-
-                vh, vm, vl = split3(assemble(base + j, h))
-                rows = pl.ds(pl.multiple_of(j * 512, 512), 512)
-                vh_s[rows, :] = vh
-                vm_s[rows, :] = vm
-                vl_s[rows, :] = vl
-                xh, xm, xl = split3(xt[8 - n + j])
-                p1 = bdot(jnp.concatenate([xh, xm, xl], axis=0), vh)
-                p2 = bdot(jnp.concatenate([xh, xm], axis=0), vm)
-                p3 = bdot(xh, vl)
-                w_s[...] += (((p3 + p1[256:]) + p2[128:]) + (p2[:128] + p1[128:256])) + p1[:128]
-
-            loop(0, n, project)
+
+            @pl.when(second == 1)
+            def _():
+                w_s[...] = jnp.zeros_like(w_s)
+                loop(0, n, project)
 
             @pl.when(second == 0)
             def _():
@@ -292,6 +306,10 @@
             y3 = jnp.concatenate([yh, ym, yl], axis=0)
 
             def update(j):
+                @pl.when(n < 8)
+                def _():
+                    share(n, (1 + 2 * second) * n + j)
+
                 rows = pl.ds(pl.multiple_of(j * 512, 512), 512)
                 d1 = ndot(y3, vh_s[rows, :])
                 d2 = ndot(y2, vm_s[rows, :])
@@ -330,7 +348,6 @@
 
 def solution(mesh):
     def local_apply(v_loc, t_loc, z_loc):
-        t2 = t_loc.reshape(8, 4, 32, 32).transpose(0, 2, 1, 3).reshape(256, 128)
         out = pl.pallas_call(
             fused_kernel,
             out_shape=jax.ShapeDtypeStruct((8, 8, 64, 128), F32),
@@ -338,6 +355,7 @@
             out_specs=pl.BlockSpec(memory_space=pl.ANY),
             scratch_shapes=[
                 pltpu.VMEM((2, 2, 2, 4, 64 * UNITS, 128), F32),
+                pltpu.VMEM((32, 32, 32), F32),
                 pltpu.VMEM((2, 2, 256, 128), F32),
                 pltpu.VMEM((8, 2, 4, 64, 128), F32),
                 pltpu.VMEM((8, 128, 512), F32),
@@ -364,7 +382,7 @@
                 collective_id=0, has_side_effects=True, vmem_limit_bytes=66 * 1000 * 1000
             ),
             name="gather_apply",
-        )(v_loc, t2, z_loc.reshape(8, 8, 64, 128))
+        )(v_loc, t_loc, z_loc.reshape(8, 8, 64, 128))
         return out.reshape(4096, 128)
 
     return jax.shard_map(

time: 196 us -> 227 us (1.16)
  Pallas kernels: 191 us -> 223 us
  local copies, waits for them, and re-layouts: 5.34 us -> 3.05 us
    pallas_call x1, Pallas kernels: 191 us -> 223 us  [local_apply(): pl.pallas_call(fused_kernel, out_shape=jax.ShapeDtypeStruct((8, 8, 64, 12...]
    reshape x2 -> x0, local copies, waits for them, and re-layouts: 2.29 us -> none  [local_apply(): t2 = t_loc.reshape(8, 4, 32, 32).transpose(0, 2, 1, 3).reshape(256, 128)]
where the time goes in v5:
time: 227 us; the launch traced here: 226 us
  Pallas kernels  223 us (98%)
  local copies, waits for them, and re-layouts  3.05 us (1%)
    pallas_call x1, Pallas kernels, local_apply(): pl.pallas_call(fused_kernel, out_shape=jax.ShapeDtypeStruct((8, 8, 64, 12...  223 us

profile of v5, /device:TPU:17, one launch (start us, length us, event | category | flops | bytes accessed | tf_op | source)
XLA Modules:
  0.0 226.4 jit_solution(258835231650446519)
XLA Ops:
  0.0 223.3 %gather_apply.1 = f32[8,8,64,128]{3,2,1,0:T(8,128)} custom-call(f32[512,1024]{1,0:T(8,128)} %v_ref.1, f32[32,32,32]{2,1,0:T(8,128)} %t_ref.1, f32[8,8,64,128]{3,2,1,0:T(8,128)} %bitcast.3), custom_call_target="tpu_custom_call" | custom-call | tf_op jit(solution)/shard_map/gather_apply/pallas_call | solution.py:351
  223.3 3.0 %copy.5 = f32[4096,128]{1,0:T(8,128)} copy(f32[4096,128]{1,0:T(8,128)} %bitcast.2) | data formatting | bytes 4194304

commit v6 on v5

--- a/solution.py
+++ b/solution.py
@@ -11,10 +11,11 @@
 HI = lax.Precision.HIGHEST
 MESH = pl.DeviceIdType.MESH
 UNITS = 36
-Z_AHEAD = 6
-D1 = 2
-D2 = 1
-D3 = 1
+Z_AHEAD = 4
+EARLY = 6
+D1 = 3
+D2 = 2
+D3 = 3
 LAG = D1 + D2 + D3
 
 
@@ -47,7 +48,7 @@
 
 
 def fused_kernel(
-    v_ref, t_ref, z_ref, o_ref, buf, traw, tbuf, stage, xt, tx, vh_s, vm_s, vl_s, g_s, a_s, w_s,
+    v_ref, t_ref, z_ref, o_ref, buf, traw, tbuf, stage, xt, tx, vh_s, vm_s, vl_s, g_s, a_s, w_s, y_s,
     in_sem, send_sem, z_sem, x1_sem, y1_sem, x2_sem, y2_sem, z2_sem, p_sem, t_sem, tx_sem,
 ):
     row, col = lax.axis_index("row"), lax.axis_index("col")
@@ -78,6 +79,10 @@
     def y1_copy(q):
         return remote(buf.at[c, x, y, :, unit(q)], y1_sem.at[q], y_dev, 2)
 
+    def xy_piece(q, k):
+        view = buf.at[c, x, y, lax.rem(slot + k, 4), unit(q)]
+        return remote(view, x1_sem.at[q], x_dev, 1), remote(view, y1_sem.at[q], y_dev, 2)
+
     def y2_copy(q):
         return remote(buf.at[c, 1 - x, y, 2 * low_z, unit(q)], y2_sem.at[q], y_dev, 3)
 
@@ -134,8 +139,18 @@
         @pl.when(q < UNITS)
         def _():
             z_land(q).wait_recv()
-            x1_copy(q).start()
-            y1_copy(q).start()
+
+            @pl.when(q < EARLY)
+            def _():
+                for k in (1, 2, 3):
+                    for copy in xy_piece(q, k):
+                        copy.start()
+
+            @pl.when(q >= EARLY)
+            def _():
+                x1_copy(q).start()
+                y1_copy(q).start()
+
             p_copy(q, x, y).start()
 
         q2 = q - D1 - D2
@@ -179,6 +194,12 @@
     pl.semaphore_wait(barrier, 6)
 
     loop(0, Z_AHEAD, z_send)
+
+    def early(q):
+        for copy in xy_piece(q, 0):
+            copy.start()
+
+    loop(0, EARLY, early)
     t_in.wait()
 
     def pack_t(b):
@@ -212,7 +233,7 @@
 
     def share(n, at):
         grow = steps(n + 1) - steps(n)
-        loop(steps(n) + at * grow // (4 * n), steps(n) + (at + 1) * grow // (4 * n), comm)
+        loop(steps(n) + at * grow // (3 * n), steps(n) + (at + 1) * grow // (3 * n), comm)
 
     def assemble(q, h):
         cols = []
@@ -242,13 +263,6 @@
             p2 = bdot(jnp.concatenate([xh, xm], axis=0), vm)
             p3 = bdot(xh, vl)
             w_s[...] += (((p3 + p1[256:]) + p2[128:]) + (p2[:128] + p1[128:256])) + p1[:128]
-
-        def project(j):
-            @pl.when(n < 8)
-            def _():
-                share(n, 2 * n + j)
-
-            apply_v(j, 0)
 
         def gram(j):
             @pl.when(n < 8)
@@ -289,36 +303,41 @@
         tx[n - 1, c] = t.T
         t_copy(n, c).start()
 
-        def half(second):
-            h = 1 - second
-
-            @pl.when(second == 1)
-            def _():
-                w_s[...] = jnp.zeros_like(w_s)
-                loop(0, n, project)
-
-            @pl.when(second == 0)
-            def _():
-                t_copy(n, 1 - c).wait_recv()
-
+        def solve(h):
             yh, ym, yl = split3(fdot(w_s[...], tx[n - 1, h]))
-            y2 = jnp.concatenate([yh, ym], axis=0)
-            y3 = jnp.concatenate([yh, ym, yl], axis=0)
-
-            def update(j):
-                @pl.when(n < 8)
-                def _():
-                    share(n, (1 + 2 * second) * n + j)
-
-                rows = pl.ds(pl.multiple_of(j * 512, 512), 512)
-                d1 = ndot(y3, vh_s[rows, :])
-                d2 = ndot(y2, vm_s[rows, :])
-                d3 = ndot(yh, vl_s[rows, :])
-                xt[8 - n + j] -= (((d3 + d1[256:]) + d2[128:]) + (d2[:128] + d1[128:256])) + d1[:128]
-
-            loop(0, n, update)
-
-        loop(0, 2, half)
+            return jnp.concatenate([yh, ym, yl], axis=0)
+
+        def update(j, y3):
+            rows = pl.ds(pl.multiple_of(j * 512, 512), 512)
+            d1 = ndot(y3, vh_s[rows, :])
+            d2 = ndot(y3[:256], vm_s[rows, :])
+            d3 = ndot(y3[:128], vl_s[rows, :])
+            xt[8 - n + j] -= (((d3 + d1[256:]) + d2[128:]) + (d2[:128] + d1[128:256])) + d1[:128]
+
+        t_copy(n, 1 - c).wait_recv()
+        y_s[...] = solve(1)
+        w_s[...] = jnp.zeros_like(w_s)
+
+        def middle(j):
+            @pl.when(n < 8)
+            def _():
+                share(n, n + j)
+
+            update(j, y_s[...])
+            apply_v(j, 0)
+
+        loop(0, n, middle)
+        y_s[...] = solve(0)
+
+        def last(j):
+            @pl.when(n < 8)
+            def _():
+                share(n, 2 * n + j)
+
+            update(j, y_s[...])
+
+        loop(0, n, last)
+
 
     loop(1, 9, pair)
 
@@ -366,6 +385,7 @@
                 pltpu.VMEM((256, 256), F32),
                 pltpu.VMEM((256, 256), F32),
                 pltpu.VMEM((128, 256), F32),
+                pltpu.VMEM((384, 256), BF16),
                 pltpu.SemaphoreType.DMA((3,)),
                 pltpu.SemaphoreType.DMA((11,)),
                 pltpu.SemaphoreType.DMA((UNITS,)),

time: 227 us -> 190 us (0.84)
  Pallas kernels: 223 us -> 186 us
    pallas_call x1, Pallas kernels: 223 us -> 186 us  [local_apply(): pl.pallas_call(fused_kernel, out_shape=jax.ShapeDtypeStruct((8, 8, 64, 12...]
where the time goes in v6:
time: 190 us; the launch traced here: 189 us
  Pallas kernels  186 us (98%)
  local copies, waits for them, and re-layouts  3.05 us (2%)
    pallas_call x1, Pallas kernels, local_apply(): pl.pallas_call(fused_kernel, out_shape=jax.ShapeDtypeStruct((8, 8, 64, 12...  186 us

profile of v6, /device:TPU:17, one launch (start us, length us, event | category | flops | bytes accessed | tf_op | source)
XLA Modules:
  0.0 189.4 jit_solution(515368394739651706)
XLA Ops:
  0.0 186.3 %gather_apply.1 = f32[8,8,64,128]{3,2,1,0:T(8,128)} custom-call(f32[512,1024]{1,0:T(8,128)} %v_ref.1, f32[32,32,32]{2,1,0:T(8,128)} %t_ref.1, f32[8,8,64,128]{3,2,1,0:T(8,128)} %bitcast.3), custom_call_target="tpu_custom_call" | custom-call | tf_op jit(solution)/shard_map/gather_apply/pallas_call | solution.py:370
  186.3 3.0 %copy.5 = f32[4096,128]{1,0:T(8,128)} copy(f32[4096,128]{1,0:T(8,128)} %bitcast.2) | data formatting | bytes 4194304

commit v7 on v6

--- a/solution.py
+++ b/solution.py
@@ -252,37 +252,52 @@
         a_s[...] = jnp.zeros_like(a_s)
         w_s[...] = jnp.zeros_like(w_s)
 
-        def apply_v(j, h):
-            vh, vm, vl = split3(assemble(base + j, h))
-            rows = pl.ds(pl.multiple_of(j * 512, 512), 512)
+        def block(j, k, h):
+            return jnp.concatenate([assemble(base + j + i, h) for i in range(k)], axis=0)
+
+        def rows_of(j, k):
+            return pl.ds(pl.multiple_of(j * 512, 512), 512 * k)
+
+        def apply_v(j, k, h):
+            vh, vm, vl = split3(block(j, k, h))
+            rows = rows_of(j, k)
             vh_s[rows, :] = vh
             vm_s[rows, :] = vm
             vl_s[rows, :] = vl
-            xh, xm, xl = split3(xt[8 - n + j])
+            xh, xm, xl = split3(jnp.concatenate([xt[8 - n + j + i] for i in range(k)], axis=1))
             p1 = bdot(jnp.concatenate([xh, xm, xl], axis=0), vh)
             p2 = bdot(jnp.concatenate([xh, xm], axis=0), vm)
             p3 = bdot(xh, vl)
             w_s[...] += (((p3 + p1[256:]) + p2[128:]) + (p2[:128] + p1[128:256])) + p1[:128]
 
-        def gram(j):
-            @pl.when(n < 8)
-            def _():
-                share(n, j)
-
-            @pl.when(n == 8)
-            def _():
-                grow = UNITS + LAG - steps(8)
-                loop(steps(8) + j * grow // 8, steps(8) + (j + 1) * grow // 8, comm)
-
-            p_land(base + j).wait_recv()
-            v = assemble(base + j, c)
+        def gram(j, k):
+            for i in range(k):
+                @pl.when(n < 8)
+                def _():
+                    share(n, j + i)
+
+                @pl.when(n == 8)
+                def _():
+                    grow = UNITS + LAG - steps(8)
+                    loop(steps(8) + (j + i) * grow // 8, steps(8) + (j + i + 1) * grow // 8, comm)
+
+            for i in range(k):
+                p_land(base + j + i).wait_recv()
+            v = block(j, k, c)
             vh, vm, vl = split3(v)
             th, tm, _ = split3(v.T)
             g_s[...] += bdot(jnp.concatenate([th, tm], axis=1), jnp.concatenate([vh, vm], axis=0))
             a_s[...] += bdot(jnp.concatenate([th, th], axis=1), jnp.concatenate([vm, vl], axis=0))
-            apply_v(j, 1)
-
-        loop(0, n, gram)
+            apply_v(j, k, 1)
+
+        def twos(body):
+            loop(0, n // 2, lambda i: body(2 * i, 2))
+
+            @pl.when(lax.rem(n, 2) == 1)
+            def _():
+                body(n - 1, 1)
+
+        twos(gram)
 
         a = a_s[...]
         g = g_s[...] + (a + a.T)
@@ -307,36 +322,40 @@
             yh, ym, yl = split3(fdot(w_s[...], tx[n - 1, h]))
             return jnp.concatenate([yh, ym, yl], axis=0)
 
-        def update(j, y3):
-            rows = pl.ds(pl.multiple_of(j * 512, 512), 512)
+        def update(j, k, y3):
+            rows = rows_of(j, k)
             d1 = ndot(y3, vh_s[rows, :])
             d2 = ndot(y3[:256], vm_s[rows, :])
             d3 = ndot(y3[:128], vl_s[rows, :])
-            xt[8 - n + j] -= (((d3 + d1[256:]) + d2[128:]) + (d2[:128] + d1[128:256])) + d1[:128]
+            d = (((d3 + d1[256:]) + d2[128:]) + (d2[:128] + d1[128:256])) + d1[:128]
+            for i in range(k):
+                xt[8 - n + j + i] -= d[:, 512 * i : 512 * i + 512]
 
         t_copy(n, 1 - c).wait_recv()
         y_s[...] = solve(1)
         w_s[...] = jnp.zeros_like(w_s)
 
-        def middle(j):
-            @pl.when(n < 8)
-            def _():
-                share(n, n + j)
-
-            update(j, y_s[...])
-            apply_v(j, 0)
-
-        loop(0, n, middle)
+        def middle(j, k):
+            for i in range(k):
+                @pl.when(n < 8)
+                def _():
+                    share(n, n + j + i)
+
+            update(j, k, y_s[...])
+            apply_v(j, k, 0)
+
+        twos(middle)
         y_s[...] = solve(0)
 
-        def last(j):
-            @pl.when(n < 8)
-            def _():
-                share(n, 2 * n + j)
-
-            update(j, y_s[...])
-
-        loop(0, n, last)
+        def last(j, k):
+            for i in range(k):
+                @pl.when(n < 8)
+                def _():
+                    share(n, 2 * n + j + i)
+
+            update(j, k, y_s[...])
+
+        twos(last)
 
 
     loop(1, 9, pair)

time: 190 us -> 185 us (0.974)
  Pallas kernels: 186 us -> 181 us
    pallas_call x1, Pallas kernels: 186 us -> 181 us  [local_apply(): pl.pallas_call(fused_kernel, out_shape=jax.ShapeDtypeStruct((8, 8, 64, 12...]
where the time goes in v7:
time: 185 us; the launch traced here: 184 us
  Pallas kernels  181 us (98%)
  local copies, waits for them, and re-layouts  3.05 us (2%)
    pallas_call x1, Pallas kernels, local_apply(): pl.pallas_call(fused_kernel, out_shape=jax.ShapeDtypeStruct((8, 8, 64, 12...  181 us

profile of v7, /device:TPU:17, one launch (start us, length us, event | category | flops | bytes accessed | tf_op | source)
XLA Modules:
  0.0 184.5 jit_solution(1926915384199760101)
XLA Ops:
  0.0 181.4 %gather_apply.1 = f32[8,8,64,128]{3,2,1,0:T(8,128)} custom-call(f32[512,1024]{1,0:T(8,128)} %v_ref.1, f32[32,32,32]{2,1,0:T(8,128)} %t_ref.1, f32[8,8,64,128]{3,2,1,0:T(8,128)} %bitcast.3), custom_call_target="tpu_custom_call" | custom-call | tf_op jit(solution)/shard_map/gather_apply/pallas_call | solution.py:389
  181.4 3.0 %copy.5 = f32[4096,128]{1,0:T(8,128)} copy(f32[4096,128]{1,0:T(8,128)} %bitcast.2) | data formatting | bytes 4194304

commit v8 on v7

--- a/solution.py
+++ b/solution.py
@@ -11,7 +11,8 @@
 HI = lax.Precision.HIGHEST
 MESH = pl.DeviceIdType.MESH
 UNITS = 36
-Z_AHEAD = 4
+Z_AHEAD = 3
+GRAM, MERGE, MIDDLE, LAST = 9, 46, 8, 4
 EARLY = 6
 D1 = 3
 D2 = 2
@@ -48,7 +49,7 @@
 
 
 def fused_kernel(
-    v_ref, t_ref, z_ref, o_ref, buf, traw, tbuf, stage, xt, tx, vh_s, vm_s, vl_s, g_s, a_s, w_s, y_s,
+    v_ref, t_ref, z_ref, o_ref, buf, traw, tbuf, stage, xt, tx, vh_s, vm_s, vl_s, g_s, a_s, w_s, y_s, t_s,
     in_sem, send_sem, z_sem, x1_sem, y1_sem, x2_sem, y2_sem, z2_sem, p_sem, t_sem, tx_sem,
 ):
     row, col = lax.axis_index("row"), lax.axis_index("col")
@@ -231,9 +232,12 @@
     def steps(n):
         return first_unit(n) + LAG + n - n // 4 - 2 * (n // 8)
 
-    def share(n, at):
-        grow = steps(n + 1) - steps(n)
-        loop(steps(n) + at * grow // (3 * n), steps(n) + (at + 1) * grow // (3 * n), comm)
+    def share(n, start, end):
+        grow, whole = steps(n + 1) - steps(n), (GRAM + MIDDLE + LAST) * n + MERGE
+
+        @pl.when(n < 8)
+        def _():
+            loop(steps(n) + start * grow // whole, steps(n) + end * grow // whole, comm)
 
     def assemble(q, h):
         cols = []
@@ -272,9 +276,7 @@
 
         def gram(j, k):
             for i in range(k):
-                @pl.when(n < 8)
-                def _():
-                    share(n, j + i)
+                share(n, GRAM * (j + i), GRAM * (j + i + 1))
 
                 @pl.when(n == 8)
                 def _():
@@ -301,8 +303,6 @@
 
         a = a_s[...]
         g = g_s[...] + (a + a.T)
-        na = 4 * (ia % 2) + ia // 2
-        nb = 4 * (ib % 2) + ib // 2
         diag = []
         t_rows = pl.ds(pl.multiple_of(32 * (8 - n), 32), 32)
         for xx in (0, 1):
@@ -311,12 +311,24 @@
                 e = jnp.where(c == cc, raw, pltpu.roll(raw, 64, 1))
                 diag += [e, e]
         t4 = jnp.concatenate(diag, axis=0)
-        t = jnp.where(ia == ib, jnp.concatenate([t4, t4], axis=1), 0.0)
-        for lev in (1, 2, 4):
-            pick = (na // (2 * lev) == nb // (2 * lev)) & ((na // lev) % 2 == 0) & ((nb // lev) % 2 == 1)
-            t = t - fdot(fdot(t, jnp.where(pick, g, 0.0)), t)
+        one = ia[:128, :128], ib[:128, :128]
+        first = (one[0] % 2 == one[1] % 2) & (one[0] // 2 == 0) & (one[1] // 2 == 1)
+        merged = []
+        for k in (0, 128):
+            d = jnp.where(one[0] == one[1], t4[k : k + 128], 0.0)
+            merged.append(d - fdot(fdot(d, jnp.where(first, g[k : k + 128, k : k + 128], 0.0)), d))
+        cross = fdot(fdot(merged[0], jnp.where(one[0] % 2 == one[1] % 2, g[:128, 128:], 0.0)), merged[1])
+        t_s[:128, :128] = merged[0]
+        t_s[:128, 128:] = -cross
+        t_s[128:, :128] = jnp.zeros((128, 128), F32)
+        t_s[128:, 128:] = merged[1]
+        g_s[...] = jnp.where((ia % 2 == 0) & (ib % 2 == 1), g, 0.0)
+        share(n, GRAM * n, GRAM * n + MERGE // 2)
+        t = t_s[...]
+        t = t - fdot(fdot(t, g_s[...]), t)
         tx[n - 1, c] = t.T
         t_copy(n, c).start()
+        share(n, GRAM * n + MERGE // 2, GRAM * n + MERGE)
 
         def solve(h):
             yh, ym, yl = split3(fdot(w_s[...], tx[n - 1, h]))
@@ -336,11 +348,8 @@
         w_s[...] = jnp.zeros_like(w_s)
 
         def middle(j, k):
-            for i in range(k):
-                @pl.when(n < 8)
-                def _():
-                    share(n, n + j + i)
-
+            start = GRAM * n + MERGE + MIDDLE * j
+            share(n, start, start + MIDDLE * k)
             update(j, k, y_s[...])
             apply_v(j, k, 0)
 
@@ -348,11 +357,8 @@
         y_s[...] = solve(0)
 
         def last(j, k):
-            for i in range(k):
-                @pl.when(n < 8)
-                def _():
-                    share(n, 2 * n + j + i)
-
+            start = (GRAM + MIDDLE) * n + MERGE + LAST * j
+            share(n, start, start + LAST * k)
             update(j, k, y_s[...])
 
         twos(last)
@@ -405,6 +411,7 @@
                 pltpu.VMEM((256, 256), F32),
                 pltpu.VMEM((128, 256), F32),
                 pltpu.VMEM((384, 256), BF16),
+                pltpu.VMEM((256, 256), F32),
                 pltpu.SemaphoreType.DMA((3,)),
                 pltpu.SemaphoreType.DMA((11,)),
                 pltpu.SemaphoreType.DMA((UNITS,)),

time: 185 us -> 175 us (0.946)
  Pallas kernels: 181 us -> 171 us
    pallas_call x1, Pallas kernels: 181 us -> 171 us  [local_apply(): pl.pallas_call(fused_kernel, out_shape=jax.ShapeDtypeStruct((8, 8, 64, 12...]
where the time goes in v8:
time: 175 us; the launch traced here: 174 us
  Pallas kernels  171 us (98%)
  local copies, waits for them, and re-layouts  3.05 us (2%)
    pallas_call x1, Pallas kernels, local_apply(): pl.pallas_call(fused_kernel, out_shape=jax.ShapeDtypeStruct((8, 8, 64, 12...  171 us

profile of v8, /device:TPU:17, one launch (start us, length us, event | category | flops | bytes accessed | tf_op | source)
XLA Modules:
  0.0 173.7 jit_solution(6103925913650783670)
XLA Ops:
  0.0 170.7 %gather_apply.1 = f32[8,8,64,128]{3,2,1,0:T(8,128)} custom-call(f32[512,1024]{1,0:T(8,128)} %v_ref.1, f32[32,32,32]{2,1,0:T(8,128)} %t_ref.1, f32[8,8,64,128]{3,2,1,0:T(8,128)} %bitcast.3), custom_call_target="tpu_custom_call" | custom-call | tf_op jit(solution)/shard_map/gather_apply/pallas_call | solution.py:395
  170.7 3.0 %copy.5 = f32[4096,128]{1,0:T(8,128)} copy(f32[4096,128]{1,0:T(8,128)} %bitcast.2) | data formatting | bytes 4194304

commit v9 on v8

--- a/solution.py
+++ b/solution.py
@@ -14,9 +14,9 @@
 Z_AHEAD = 3
 GRAM, MERGE, MIDDLE, LAST = 9, 46, 8, 4
 EARLY = 6
-D1 = 3
+D1 = 2
 D2 = 2
-D3 = 3
+D3 = 2
 LAG = D1 + D2 + D3
 
 

time: 175 us -> 174 us (level)
  no operation moved by 1% of the time
where the time goes in v9:
time: 174 us
  Pallas kernels  171 us (98%)
  local copies, waits for them, and re-layouts  3.05 us (2%)
    pallas_call x1, Pallas kernels, local_apply(): pl.pallas_call(fused_kernel, out_shape=jax.ShapeDtypeStruct((8, 8, 64, 12...  171 us

profile of v9, /device:TPU:17, one launch (start us, length us, event | category | flops | bytes accessed | tf_op | source)
XLA Modules:
  0.0 174.0 jit_solution(12969754228780115202)
XLA Ops:
  0.0 170.9 %gather_apply.1 = f32[8,8,64,128]{3,2,1,0:T(8,128)} custom-call(f32[512,1024]{1,0:T(8,128)} %v_ref.1, f32[32,32,32]{2,1,0:T(8,128)} %t_ref.1, f32[8,8,64,128]{3,2,1,0:T(8,128)} %bitcast.3), custom_call_target="tpu_custom_call" | custom-call | tf_op jit(solution)/shard_map/gather_apply/pallas_call | solution.py:395
  170.9 3.0 %copy.5 = f32[4096,128]{1,0:T(8,128)} copy(f32[4096,128]{1,0:T(8,128)} %bitcast.2) | data formatting | bytes 4194304

commit v10 on v9

--- a/solution.py
+++ b/solution.py
@@ -366,15 +366,10 @@
 
     loop(1, 9, pair)
 
-    def turn_out(u):
-        stage[u] = xt[u].T.reshape(2, 4, 64, 128)
-
-        def z_out(r):
-            pltpu.make_async_copy(stage.at[u, lax.rem(r, 2), place(r)], o_ref.at[r, u], in_sem.at[1]).start()
-
-        loop(0, 8, z_out)
-
-    loop(0, 8, turn_out)
+    def x_out(u):
+        return pltpu.make_async_copy(xt.at[u], o_ref.at[u], in_sem.at[1])
+
+    loop(0, 8, lambda u: x_out(u).start())
 
     remote(buf.at[c, x, y, 0:3], z_sem.at[0], x_dev, 0).wait_send()
     remote(buf.at[c, x, y], x1_sem.at[0], x_dev, 1).wait_send()
@@ -387,14 +382,22 @@
     t_p[0].wait_send()
     t_p[1].wait_send()
     remote(tx.at[:, 0], tx_sem.at[0], p_dev, 10).wait_send()
-    pltpu.make_async_copy(stage, stage, in_sem.at[1]).wait()
+    pltpu.make_async_copy(xt, xt, in_sem.at[1]).wait()
+
+
+def turn_kernel(x_ref, o_ref):
+    for u in range(2):
+        rows = x_ref[u].T
+        for r in range(8):
+            at = 64 * (4 * (r % 2) + 2 * (r // 2 % 2) + r // 4)
+            o_ref[r, u] = rows[at : at + 64]
 
 
 def solution(mesh):
     def local_apply(v_loc, t_loc, z_loc):
         out = pl.pallas_call(
             fused_kernel,
-            out_shape=jax.ShapeDtypeStruct((8, 8, 64, 128), F32),
+            out_shape=jax.ShapeDtypeStruct((8, 128, 512), F32),
             in_specs=[pl.BlockSpec(memory_space=pl.ANY)] * 3,
             out_specs=pl.BlockSpec(memory_space=pl.ANY),
             scratch_shapes=[
@@ -429,7 +432,15 @@
             ),
             name="gather_apply",
         )(v_loc, t_loc, z_loc.reshape(8, 8, 64, 128))
-        return out.reshape(4096, 128)
+        turned = pl.pallas_call(
+            turn_kernel,
+            grid=(4,),
+            out_shape=jax.ShapeDtypeStruct((8, 8, 64, 128), F32),
+            in_specs=[pl.BlockSpec((2, 128, 512), lambda u: (u, 0, 0))],
+            out_specs=pl.BlockSpec((8, 2, 64, 128), lambda u: (0, u, 0, 0)),
+            name="turn",
+        )(out)
+        return turned.reshape(4096, 128)
 
     return jax.shard_map(
         local_apply,

time: 174 us -> 174 us (level)
  local copies, waits for them, and re-layouts: 3.05 us -> 0 us
  Pallas kernels: 171 us -> 174 us
    unnamed x1 -> x0, local copies, waits for them, and re-layouts: 3.05 us -> none
    pallas_call x1 -> x2, Pallas kernels: 171 us -> 174 us  [the longest x1 170 us: local_apply(): pl.pallas_call(fused_kernel, out_shape=jax.ShapeDtypeStruct((8, 128, 512)...]
where the time goes in v10:
time: 174 us
  Pallas kernels  174 us (100%)
    pallas_call x1, Pallas kernels, local_apply(): pl.pallas_call(fused_kernel, out_shape=jax.ShapeDtypeStruct((8, 128, 512)...  170 us
    pallas_call x1, Pallas kernels, local_apply(): pl.pallas_call(turn_kernel, grid=(4,), out_shape=jax.ShapeDtypeStruct((8,...  4.12 us

profile of v10, /device:TPU:17, one launch (start us, length us, event | category | flops | bytes accessed | tf_op | source)
XLA Modules:
  0.0 173.8 jit_solution(14208619231814356194)
XLA Ops:
  0.0 169.6 %gather_apply.1.x_ref = f32[8,128,512]{2,1,0:T(8,128)} custom-call(f32[512,1024]{1,0:T(8,128)} %v_ref.1, f32[32,32,32]{2,1,0:T(8,128)} %t_ref.1, f32[8,8,64,128]{3,2,1,0:T(8,128)} %bitcast.2), custom_call_target="tpu_custom_call" | custom-call | tf_op jit(solution)/shard_map/gather_apply/pallas_call | solution.py:398
  169.7 4.1 %turn.1 = f32[8,8,64,128]{3,2,1,0:T(8,128)} custom-call(f32[8,128,512]{2,1,0:T(8,128)} %gather_apply.1.x_ref), custom_call_target="tpu_custom_call" | custom-call | tf_op jit(solution)/shard_map/turn/pallas_call | solution.py:435
